TPU v7x, 512 devices: a whole 4x4x16 slice. The times are simulated.
512 devices in a mesh: pb: 16 (over x, y_lo, core), dev: 32 (over z, y_hi).
Axes of the slice: x: 4, y: 4 (y_hi: 2, y_lo: 2; y = y_hi * 2 + y_lo), z: 16, core: 2. Of those that a mesh axis runs over, the one named last changes fastest.
Arguments:
- queries: bfloat16 [1024, 768], P(('pb', 'dev')), may hold values from -6 to 6
- probes: int32 [1024, 16], P(('pb', 'dev')), may hold values from 0 to 1023, all different within a row
- vectors: bfloat16 [262144, 768], P(('pb', 'dev')), may hold values from -0.4375 to 0.4375
- list_ids: int32 [262144], P(('pb', 'dev')), may hold values from 0 to 1023, as said below
Outputs:
- leaders: float32 [1024, 100], P(('pb', 'dev'))
Inputs may be any that keep to these rules, and one draw needn't show every extreme that they name: `list_ids`: each list id names exactly 256 database vectors. `probes`: each query names 16 different lists.
All inputs are finite; a program needn't handle non-finite values.
Results may differ from a plain program's by a relative error of at most 0.0004.
Values may be sent and summed in bfloat16 or wider, within the bound.
A program may use at most 64 MiB of HBM per device.

v0:
```python
import math

import jax
import jax.numpy as jnp
from jax import lax
from jax.sharding import PartitionSpec as P

K = 100
NLIST = 1024


masked_value = -1e30


def split_up(value, dim, size):
    before, after = (value.shape[:dim], value.shape[dim + 1 :])
    return jnp.moveaxis(value.reshape(*before, size, -1, *after), dim, 0)


def joined_along(blocks, dim):
    lengths = list(blocks.shape[1:])
    lengths[dim] *= blocks.shape[0]
    return jnp.moveaxis(blocks, 0, dim).reshape(lengths)


def joined_exchange(value, axis, axes, splits, concats):
    sizes = [lax.axis_size(a) for a in axes]
    blocks = split_up(value, splits[0], sizes[0])
    blocks = jnp.moveaxis(split_up(blocks, splits[1] + 1, sizes[1]), 0, 1)
    inside = blocks.shape[2:]
    blocks = blocks.reshape(-1, *inside)
    blocks = lax.all_to_all(blocks, axis, split_axis=0, concat_axis=0, tiled=True)
    blocks = joined_along(blocks.reshape(*sizes, *inside), concats[0] + 1)
    return joined_along(blocks, concats[1])


def filtered_scores(block_rows, block_probes, slab_part, list_onehot):
    products = lax.dot_general(
        block_rows, slab_part, (((1,), (1,)), ((), ())), preferred_element_type=jnp.float32
    )
    count = block_rows.shape[0]
    row_index = lax.broadcasted_iota(jnp.int32, block_probes.shape, 0)
    hits = (
        jnp.zeros((count, list_onehot.shape[0]), jnp.bfloat16)
        .at[row_index, block_probes]
        .set(jnp.bfloat16(1.0))
    )
    matches = jnp.dot(hits, list_onehot, preferred_element_type=jnp.float32)
    return jnp.where(matches > 0.5, products, jnp.float32(masked_value))


def local(queries, probes, vectors, list_ids):
    local_count = min(K, vectors.shape[0])
    list_index = lax.broadcasted_iota(jnp.int32, (NLIST, list_ids.shape[0]), 0)
    list_onehot = (list_index == list_ids[None, :]).astype(jnp.bfloat16)
    block_rows, block_probes = lax.all_gather((queries, probes), ("pb", "dev"), axis=0, tiled=True)
    count = block_rows.shape[0]
    width = math.gcd(count, 256)

    def one_block(block_args):
        rows_here, probes_here = block_args
        kept, _ = lax.top_k(
            filtered_scores(rows_here, probes_here, vectors, list_onehot), local_count
        )
        return kept

    kept = lax.map(
        one_block,
        (
            block_rows.reshape(count // width, width, block_rows.shape[1]),
            block_probes.reshape(count // width, width, block_probes.shape[1]),
        ),
    )
    candidates = kept.reshape(count, local_count)
    pooled = joined_exchange(candidates, ("pb", "dev"), ("pb", "dev"), (0, 0), (1, 1))
    leaders, _ = lax.top_k(pooled, K)
    return leaders


def solution(mesh):
    return jax.shard_map(
        local,
        mesh=mesh,
        in_specs=(
            P(("pb", "dev"), None),
            P(("pb", "dev"), None),
            P(("pb", "dev"), None),
            P(("pb", "dev")),
        ),
        out_specs=P(("pb", "dev"), None),
        check_vma=False,
    )
```

profile of v0, /device:TPU:1, one launch (start us, length us, event | category | flops | bytes accessed | tf_op | source)
XLA Modules:
  0.0 1552.7 jit_solution(2833218689771268796)
XLA Ops:
  6.5 0.7 all-gather.4.cloned.1.call-update
  7.3 1215.8 %all-gather = s32[512,2,16]{2,1,0:T(2,128)S(1)} all-gather(s32[1,2,16]{2,1,0:T(2,128)} %bitcast.40), channel_id=1, replica_groups=mesh['pb'=16,'dev'=32] {'pb','dev'}, dimensions={0}, use_global_device_ids=true | all-gather | bytes 65664 | tf_op jit(solution)/shard_map/all_gather | solution.py:56
  1223.2 4.7 reshape.57
  1228.0 187.0 %while.11 = (s32[]{:T(128)}, f32[4,256,100]{2,1,0:T(8,128)S(1)}, s32[4,256,16]{1,2,0:T(8,128)S(1)}, bf16[4,256,768]{2,1,0:T(8,128)(2,1)}, bf16[512,768]{1,0:T(8,...) while((s32[]{:T(128)}, f32[4,256,100]{2,1,0:T(8,128)S(1)}, ...), condition=%wide.region_3.4_spmd.clone, body=%wide.region_0.3_spmd.clone.sunk | while | flops 473374720 | bytes 9292425 | solution.py:67
  1228.4 28.8 %scatter_custom_fusion.6 = bf16[262144]{0:T(1024)(128)(2,1)S(1)} fusion(s32[4096]{0:T(1024)S(1)} %reshape.89, bf16[4096]{0:T(1024)(128)(2,1)S(1)} %broadcast.103, bf16[]{:T(256)} %constant.30.clone.2..sunk), kind=kCustom, calls=%fused_computation.9.clone.1 | custom fusion | bytes 524290 | tf_op jit(solution)/shard_map/while
  1257.2 0.2 reshape.90
  1257.5 0.4 convolution_compare_fusion.2
  1257.9 1.4 convolution_select_fusion.2
  1259.3 0.2 copy.22
  1259.6 15.0 top_k.30
  1275.2 28.8 %scatter_custom_fusion.6 = bf16[262144]{0:T(1024)(128)(2,1)S(1)} fusion(s32[4096]{0:T(1024)S(1)} %reshape.89, bf16[4096]{0:T(1024)(128)(2,1)S(1)} %broadcast.103, bf16[]{:T(256)} %constant.30.clone.2..sunk), kind=kCustom, calls=%fused_computation.9.clone.1 | custom fusion | bytes 524290 | tf_op jit(solution)/shard_map/while
  1304.0 0.2 reshape.90
  1304.2 0.4 convolution_compare_fusion.2
  1304.7 1.4 convolution_select_fusion.2
  1306.1 0.2 copy.22
  1306.3 15.0 top_k.30
  1322.0 28.8 %scatter_custom_fusion.6 = bf16[262144]{0:T(1024)(128)(2,1)S(1)} fusion(s32[4096]{0:T(1024)S(1)} %reshape.89, bf16[4096]{0:T(1024)(128)(2,1)S(1)} %broadcast.103, bf16[]{:T(256)} %constant.30.clone.2..sunk), kind=kCustom, calls=%fused_computation.9.clone.1 | custom fusion | bytes 524290 | tf_op jit(solution)/shard_map/while
  1350.8 0.2 reshape.90
  1351.0 0.4 convolution_compare_fusion.2
  1351.4 1.4 convolution_select_fusion.2
  1353.1 15.0 top_k.30
  1368.7 28.8 %scatter_custom_fusion.6 = bf16[262144]{0:T(1024)(128)(2,1)S(1)} fusion(s32[4096]{0:T(1024)S(1)} %reshape.89, bf16[4096]{0:T(1024)(128)(2,1)S(1)} %broadcast.103, bf16[]{:T(256)} %constant.30.clone.2..sunk), kind=kCustom, calls=%fused_computation.9.clone.1 | custom fusion | bytes 524290 | tf_op jit(solution)/shard_map/while
  1397.5 0.2 reshape.90
  1397.7 0.4 convolution_compare_fusion.2
  1398.2 1.4 convolution_select_fusion.2
  1399.6 0.2 copy.22
  1399.9 15.0 top_k.30
  1415.1 83.2 %all_to_all.5 = f32[512,2,100]{2,1,0:T(2,128)S(1)} all-to-all(f32[512,2,100]{2,1,0:T(2,128)S(1)} %bitcast.38), channel_id=1, replica_groups=mesh['pb'=16,'dev'=32] {'pb','dev'}, dimensions={0} | all-to-all | bytes 819200 | tf_op jit(solution)/shard_map/all_to_all | solution.py:32
  1498.2 0.3 copy.17
  1498.5 0.3 reshape.59
  1498.8 0.4 reshape.60
  1499.2 46.7 %top_k.17 = (f32[2,100]{1,0:T(2,128)}, s32[2,100]{1,0:T(2,128)}) custom-call(f32[2,51200]{1,0:T(2,128)S(1)} %reshape.60), custom_call_target="TopK", called_computations={%compare_greater_than.0.5.clone.clone} | custom-call | tf_op jit(solution)/shard_map/top_k | solution.py:76
  (57 shorter events, 2.9 us)
Async XLA Ops:
  6.5 1216.7 %all-gather.4.cloned.1.call-start = ((), (), s32[]{:S(2)}) async-start(), calls=%async_computation.1 | async-start | bytes 1575936 | tf_op jit(solution)/shard_map/all_gather | solution.py:56
  1223.2 4.8 copy-start
  1223.2 4.8 copy-start.1
  1223.2 4.8 copy-start.2
  1223.2 4.8 copy-start.3
Sparse Core Ops, SparseCore 0:
  9.5 1087.1 all-gather.3
where the time goes:
time: 1550 us
  blocking collectives  1300 us (84%)
  local copies, waits for them, and re-layouts  125 us (8%)
  other arithmetic  107 us (7%)
    all_gather x1, blocking collectives, local(): lax.all_gather((queries, probes), ('pb', 'dev'), axis=0, tiled=True)  1220 us
    while x20, local copies, waits for them, and re-layouts  117 us
    all_to_all x1, blocking collectives, joined_exchange(): lax.all_to_all(blocks, axis, split_axis=0, concat_axis=0, tiled=True)  83.2 us
    top_k x4, other arithmetic, one_block(): lax.top_k(filtered_scores(rows_here, probes_here, vectors, list_onehot),...  59.8 us
    top_k x1, other arithmetic, local(): leaders, _ = lax.top_k(pooled, K)  46.7 us
  transfers between devices with their start and end apart: 1, of which 0 were waited for; matrix products, arithmetic and copies ran while one was open for 0% of the time, Pallas kernels for 0%

commit v1 on v0

v1 whole, which is shorter than its diff:
```python
import functools

import jax
import jax.numpy as jnp
from jax import lax
from jax.experimental import pallas as pl
from jax.experimental.pallas import tpu as pltpu
from jax.sharding import PartitionSpec as P

K = 100
SENT = 104
NEG = -1.0e30
MESH = pl.DeviceIdType.MESH
F32 = jnp.float32


def exchange(a, b):
    return jnp.maximum(a, b), jnp.minimum(a, b)


def sort_desc(xs):
    xs, n, p = list(xs), len(xs), 1
    while p < n:
        k = p
        while k >= 1:
            for j in range(k % p, n - k, 2 * k):
                for i in range(min(k, n - j - k)):
                    if (i + j) // (2 * p) == (i + j + k) // (2 * p):
                        xs[i + j], xs[i + j + k] = exchange(xs[i + j], xs[i + j + k])
            k //= 2
        p *= 2
    return xs


def clean_desc(xs):
    xs, d = list(xs), len(xs) // 2
    while d >= 1:
        for i in range(len(xs)):
            if i & d == 0:
                xs[i], xs[i + d] = exchange(xs[i], xs[i + d])
        d //= 2
    return xs


def merge_top(load_a, load_b, tmp_load, tmp_store, store):
    @pl.loop(0, 8)
    def _(g):
        for u in range(4):
            i = g * 4 + u
            m = [jnp.maximum(load_a(i + 32 * k), load_b(127 - i - 32 * k)) for k in range(4)]
            m[0], m[2] = exchange(m[0], m[2])
            m[1], m[3] = exchange(m[1], m[3])
            m[0], m[1] = exchange(m[0], m[1])
            m[2], m[3] = exchange(m[2], m[3])
            for k in range(4):
                tmp_store(i + 32 * k, m[k])

    @pl.loop(0, 4)
    def _(k):
        xs = clean_desc([tmp_load(32 * k + i) for i in range(32)])
        for i in range(32):
            store(32 * k + i, xs[i])


def kernel(
    q_ref, p_ref, v_hbm, id_ref, o_ref,
    zbuf, gath, v_vm, prod, words, codes, runs, runs2, csend, crecv, ctmp,
    xsend, xrecv, atmp, apair, row_a, row_b, row_c, ysend, yrecv, zsend, zrecv,
    v_sem, zs, zr, fs, fr, ss, sr, cs, cr, rcs, rcr, rxs, rxr, rys, ryr, rzs, rzr,
):
    pb, dev = lax.axis_index("pb"), lax.axis_index("dev")
    x, ylo, c = pb // 4, (pb // 2) % 2, pb % 2
    z, yhi = dev // 2, dev % 2
    y = yhi * 2 + ylo

    def at(x_, y_, z_, c_):
        return {"pb": x_ * 4 + (y_ % 2) * 2 + c_, "dev": z_ * 2 + y_ // 2}

    z_peers = [at(x, y, (z + k) % 16, c) for k in range(1, 16)]
    y_peers = [at(x, (y + k) % 4, z, c) for k in range(1, 4)]
    x_peers = [at((x + k) % 4, y, z, c) for k in range(1, 4)]
    partner = at(x, y, z, 1 - c)

    barrier = pltpu.get_barrier_semaphore()
    everyone = z_peers + y_peers + x_peers + [partner]
    for peer in everyone:
        pl.semaphore_signal(barrier, inc=1, device_id=peer, device_id_type=MESH)

    v_copy = pltpu.make_async_copy(v_hbm, v_vm, v_sem)
    v_copy.start()

    zbuf[z, 12:16, :] = jnp.zeros((4, 128), jnp.bfloat16)
    for i in range(6):
        zbuf[z, 2 * i : 2 * i + 2, :] = q_ref[:, 128 * i : 128 * i + 128]
    lists = p_ref[...]
    zbuf[z, 12:14, 0:16] = (lists // 32).astype(F32).astype(jnp.bfloat16)
    zbuf[z, 12:14, 16:32] = (lists % 32).astype(F32).astype(jnp.bfloat16)
    for ref in (crecv, ):
        ref[...] = jnp.full(ref.shape, NEG, F32)
    for s in range(4):
        xrecv[s * 128 + SENT : s * 128 + 128, :] = jnp.full((128 - SENT, 128), NEG, F32)

    pl.semaphore_wait(barrier, len(everyone))

    def remote(src, dst, send, recv, peer):
        copy = pltpu.make_async_remote_copy(
            src_ref=src, dst_ref=dst, send_sem=send, recv_sem=recv,
            device_id=peer, device_id_type=MESH,
        )
        copy.start()
        return copy

    sent = []
    z_copies = [
        remote(zbuf.at[z], zbuf.at[z], zs.at[k], zr.at[k], z_peers[k]) for k in range(15)
    ]
    sent += z_copies
    r = lax.broadcasted_iota(jnp.int32, (224, 256), 0)
    k_ = lax.broadcasted_iota(jnp.int32, (224, 256), 1)
    pick = k_ == ((r % 32) // 2) * 16 + (r // 32) * 2 + r % 2
    pick = jnp.where(pick, 1.0, 0.0).astype(jnp.bfloat16)
    for copy in z_copies:
        copy.wait_recv()
    rows = jnp.dot(pick, zbuf[...].reshape(256, 128), preferred_element_type=F32)
    rows = rows.astype(jnp.bfloat16)
    for h in range(2):
        for i in range(7):
            gath[c, x, y, h, :, 128 * i : 128 * i + 128] = rows[
                32 * i + 16 * h : 32 * i + 16 * h + 16, :
            ]

    def piece(h, back1, back2):
        if h == 0:
            return gath.at[c, (x + 4 - back2) % 4, (y + 4 - back1) % 4, h]
        return gath.at[c, (x + 4 - back1) % 4, (y + 4 - back2) % 4, h]

    peers1 = [y_peers, x_peers]
    peers2 = [x_peers, y_peers]
    first, second, cross = {}, {}, {}
    for k in range(3):
        for h in range(2):
            ref = piece(h, 0, 0)
            first[h, k] = remote(ref, ref, fs.at[h, k], fr.at[h, k], peers1[h][k])

    def forward2(h, b):
        ref = piece(h, b, 0)
        for k in range(3):
            second[h, b, k] = remote(ref, ref, ss.at[h, b, k], sr.at[h, b, k], peers2[h][k])

    def forward_core(h, b1, b2):
        ref, n = piece(h, b1, b2), b1 * 4 + b2
        cross[h, b1, b2] = remote(ref, ref, cs.at[h, n], cr.at[h, n], partner)

    for h in range(2):
        forward2(h, 0)
    for h in range(2):
        forward_core(h, 0, 0)
    for b in (1, 3, 2):
        for h in range(2):
            first[h, b - 1].wait_recv()
            forward2(h, b)
            forward_core(h, b, 0)
    for b1 in (0, 1, 3, 2):
        for b2 in (1, 3, 2):
            for h in range(2):
                second[h, b1, b2 - 1].wait_recv()
                forward_core(h, b1, b2)
    sent += list(first.values()) + list(second.values()) + list(cross.values())
    for copy in cross.values():
        copy.wait_recv()
    v_copy.wait()

    for s in range(8):
        part = gath[s // 4, s % 4].reshape(128, 896)[:, 768:896]
        turned = part.astype(F32).T
        codes[32 * s : 32 * s + 32, :] = turned[:32, :].astype(jnp.int32)

    @pl.loop(0, 4)
    def _(s2):
        block = gath[s2 // 2, pl.ds((s2 % 2) * 2, 2)].reshape(256, 896)[:, :768]
        for m in range(4):
            scores = lax.dot_general(
                v_vm[128 * m : 128 * m + 128, :], block,
                (((1,), (1,)), ((), ())), preferred_element_type=F32,
            )
            for j in range(16):
                for t in range(2):
                    row = pl.multiple_of((16 * m + j) * 64 + (s2 * 2 + t) * 8, 8)
                    prod[pl.ds(row, 8), :] = scores[8 * j : 8 * j + 8, 128 * t : 128 * t + 128]

    high = [codes[pl.ds(p, 8, stride=32), :] for p in range(16)]
    bits = [jnp.left_shift(jnp.int32(1), codes[pl.ds(16 + p, 8, stride=32), :]) for p in range(16)]

    @pl.loop(0, 32)
    def _(a):
        word = jnp.zeros((8, 128), jnp.int32)
        for p in range(16):
            word = word | jnp.where(high[p] == a, bits[p], 0)
        words[a] = word

    @pl.loop(0, 16)
    def _(g):
        xs = []
        for i in range(32):
            value = prod[pl.ds(g * 256 + (i // 8) * 64 + i % 8, 8, stride=8), :]
            which = id_ref[g * 32 + i]
            word = words[which // 32]
            keep = (word & jnp.left_shift(jnp.int32(1), which % 32)) != 0
            xs.append(jnp.where(keep, value, NEG))
        xs = sort_desc(xs)
        for i in range(32):
            runs[g * 32 + i] = xs[i]

    @pl.loop(0, 8)
    def _(g):
        base = g * 64
        for side, op in ((0, jnp.maximum), (1, jnp.minimum)):
            xs = [op(runs[base + i], runs[base + 63 - i]) for i in range(32)]
            xs = clean_desc(xs)
            for i in range(32):
                runs2[base + 32 * side + i] = xs[i]

    @pl.loop(0, 4)
    def _(g):
        base = g * 128
        for i in range(32):
            a, b = runs2[base + i], runs2[base + 127 - i]
            a2, b2 = runs2[base + 32 + i], runs2[base + 95 - i]
            h1, l1 = exchange(a, b)
            h2, l2 = exchange(a2, b2)
            h1, h2 = exchange(h1, h2)
            l1, l2 = exchange(l1, l2)
            runs[base + i], runs[base + 32 + i] = h1, h2
            runs[base + 64 + i], runs[base + 96 + i] = l1, l2

    @pl.loop(0, 16)
    def _(g):
        xs = clean_desc([runs[g * 32 + i] for i in range(32)])
        for i in range(32):
            runs2[g * 32 + i] = xs[i]

    def run_store(ref, base):
        def put(i, value):
            ref[base + i] = value
        return put

    def run_load(ref, base):
        return lambda i: ref[base + i]

    for g in range(2):
        merge_top(
            run_load(runs2, 256 * g), run_load(runs2, 256 * g + 128),
            run_load(runs, 256 * g), run_store(runs, 256 * g), run_store(runs2, 256 * g),
        )

    def split_store(i, value):
        csend[0, i] = value[0:4, :]
        csend[1, i] = value[4:8, :]

    merge_top(run_load(runs2, 0), run_load(runs2, 256), run_load(runs, 0), run_store(runs, 0), split_store)

    copy = remote(
        csend.at[1 - c, pl.ds(0, SENT)], crecv.at[pl.ds(0, SENT)], rcs.at[0], rcr.at[0], partner
    )
    sent.append(copy)
    copy.wait_recv()

    def x_store(i, value):
        xsend[pl.ds(i, 4, stride=128), :] = value

    merge_top(lambda i: csend[c, i], run_load(crecv, 0), run_load(ctmp, 0), run_store(ctmp, 0), x_store)

    def x_rows(s):
        return pl.ds(pl.multiple_of(s * 128, 128), SENT)

    copies = [
        remote(
            xsend.at[x_rows((x + k + 1) % 4)], xrecv.at[x_rows(x)],
            rxs.at[k], rxr.at[k], x_peers[k],
        )
        for k in range(3)
    ]
    sent += copies
    xrecv[x_rows(x), :] = xsend[x_rows(x), :]
    for copy in copies:
        copy.wait_recv()

    def pair_store(i, value):
        apair[pl.ds(i, 2, stride=128), :] = value

    merge_top(
        lambda i: xrecv[pl.ds(i, 2, stride=128), :], lambda i: xrecv[pl.ds(256 + i, 2, stride=128), :],
        run_load(atmp, 0), run_store(atmp, 0), pair_store,
    )

    def row_load(ref, base=0):
        return lambda i: ref[pl.ds(base + i, 1), :]

    def row_store(ref):
        def put(i, value):
            ref[pl.ds(i, 1), :] = value
        return put

    merge_top(row_load(apair), row_load(apair, 128), row_load(row_c), row_store(row_c), row_store(row_a))

    def fold_lanes(distance):
        row_b[...] = pltpu.roll(row_a[...], 128 - distance, axis=1)
        merge_top(row_load(row_a), row_load(row_b), row_load(row_c), row_store(row_c), row_store(row_a))

    ysend[...] = row_a[...].T

    def y_rows(s):
        return pl.ds(pl.multiple_of(s * 32, 32), 32)

    copies = [
        remote(
            ysend.at[y_rows((y + k + 1) % 4)], yrecv.at[y_rows(y)],
            rys.at[k], ryr.at[k], y_peers[k],
        )
        for k in range(3)
    ]
    sent += copies
    yrecv[y_rows(y), :] = ysend[y_rows(y), :]
    for copy in copies:
        copy.wait_recv()
    row_a[...] = yrecv[...].T
    fold_lanes(64)
    fold_lanes(32)

    turned = row_a[...].T
    for s in range(16):
        zsend[s] = turned[2 * s : 2 * s + 2, :]
    copies = [
        remote(zsend.at[(z + k + 1) % 16], zrecv.at[z], rzs.at[k], rzr.at[k], z_peers[k])
        for k in range(15)
    ]
    sent += copies
    zrecv[z] = zsend[z]
    for copy in copies:
        copy.wait_recv()
    row_b[32:128, :] = jnp.full((96, 128), NEG, F32)
    for s in range(16):
        row_b[2 * s : 2 * s + 2, :] = zrecv[s]
    row_a[...] = row_b[...].T
    for distance in (16, 8, 4, 2):
        fold_lanes(distance)
    o_ref[...] = row_a[...].T[0:2, 0:K]

    for copy in sent:
        copy.wait_send()


def local(queries, probes, vectors, list_ids):
    vmem = pl.BlockSpec(memory_space=pltpu.VMEM)
    dma = pltpu.SemaphoreType.DMA
    return pl.pallas_call(
        kernel,
        out_shape=jax.ShapeDtypeStruct((2, K), F32),
        in_specs=[
            vmem, vmem, pl.BlockSpec(memory_space=pl.ANY), pl.BlockSpec(memory_space=pltpu.SMEM),
        ],
        out_specs=vmem,
        scratch_shapes=[
            pltpu.VMEM((16, 16, 128), jnp.bfloat16),
            pltpu.VMEM((2, 4, 4, 2, 16, 896), jnp.bfloat16),
            pltpu.VMEM((512, 768), jnp.bfloat16),
            pltpu.VMEM((4096, 128), F32),
            pltpu.VMEM((32, 8, 128), jnp.int32),
            pltpu.VMEM((256, 128), jnp.int32),
            pltpu.VMEM((512, 8, 128), F32),
            pltpu.VMEM((512, 8, 128), F32),
            pltpu.VMEM((2, 128, 4, 128), F32),
            pltpu.VMEM((128, 4, 128), F32),
            pltpu.VMEM((128, 4, 128), F32),
            pltpu.VMEM((512, 128), F32),
            pltpu.VMEM((512, 128), F32),
            pltpu.VMEM((128, 2, 128), F32),
            pltpu.VMEM((256, 128), F32),
            pltpu.VMEM((128, 128), F32),
            pltpu.VMEM((128, 128), F32),
            pltpu.VMEM((128, 128), F32),
            pltpu.VMEM((128, 128), F32),
            pltpu.VMEM((128, 128), F32),
            pltpu.VMEM((16, 2, 128), F32),
            pltpu.VMEM((16, 2, 128), F32),
            dma, dma((15,)), dma((15,)), dma((2, 3)), dma((2, 3)), dma((2, 4, 3)), dma((2, 4, 3)),
            dma((2, 16)), dma((2, 16)), dma((1,)), dma((1,)), dma((3,)), dma((3,)),
            dma((3,)), dma((3,)), dma((15,)), dma((15,)),
        ],
        compiler_params=pltpu.CompilerParams(collective_id=0, has_side_effects=True),
    )(queries, probes, vectors, list_ids)


def solution(mesh):
    return jax.shard_map(
        local,
        mesh=mesh,
        in_specs=(
            P(("pb", "dev"), None),
            P(("pb", "dev"), None),
            P(("pb", "dev"), None),
            P(("pb", "dev")),
        ),
        out_specs=P(("pb", "dev"), None),
        check_vma=False,
    )
```

time: 1550 us -> 68.5 us (0.04)
  the two profiles are of different devices: /device:TPU:1 before, /device:TPU:8 now
where the time goes in v1:
time: 68.5 us; the launch traced here: 68.4 us
  Pallas kernels  67.1 us (98%)
  local copies, waits for them, and re-layouts  1.24 us (2%)
    pallas_call x1, Pallas kernels, local(): pl.pallas_call(kernel, out_shape=jax.ShapeDtypeStruct((2, K), F32), in_sp...  67.1 us

profile of v1, /device:TPU:8, one launch (start us, length us, event | category | flops | bytes accessed | tf_op | source)
XLA Modules:
  0.0 68.4 jit_solution(5299717646536230542)
XLA Ops:
  0.0 67.1 %shard_map.46 = f32[2,100]{1,0:T(2,128)} custom-call(bf16[2,768]{1,0:T(2,128)(2,1)} %q_ref.1, s32[2,16]{1,0:T(2,128)} %p_ref.1, bf16[512,768]{1,0:T(8,128)(2,1)} %v_hbm.1, s32[512]{0:T(512)} %id_ref.1), custom_call_target="tpu_custom_call" | custom-call | tf_op jit(solution)/shard_map/pallas_call | solution.py:356
  67.1 1.2 %copy.6 = f32[2,100]{1,0:T(2,128)} copy(f32[2,100]{1,0:T(2,128)} %shard_map.46) | data formatting | bytes 1600

commit v2 on v1

--- a/solution.py
+++ b/solution.py
@@ -63,10 +63,10 @@
 
 
 def kernel(
-    q_ref, p_ref, v_hbm, id_ref, o_ref,
-    zbuf, gath, v_vm, prod, words, codes, runs, runs2, csend, crecv, ctmp,
+    q_hbm, p_hbm, v_hbm, id_hbm, o_ref,
+    q_ref, p_ref, id_ref, zbuf, gath, v_vm, prod, words, codes, runs, runs2, csend, crecv, ctmp,
     xsend, xrecv, atmp, apair, row_a, row_b, row_c, ysend, yrecv, zsend, zrecv,
-    v_sem, zs, zr, fs, fr, ss, sr, cs, cr, rcs, rcr, rxs, rxr, rys, ryr, rzs, rzr,
+    in_sem, zs, zr, fs, fr, ss, sr, cs, cr, rcs, rcr, rxs, rxr, rys, ryr, rzs, rzr,
 ):
     pb, dev = lax.axis_index("pb"), lax.axis_index("dev")
     x, ylo, c = pb // 4, (pb // 2) % 2, pb % 2
@@ -76,30 +76,38 @@
     def at(x_, y_, z_, c_):
         return {"pb": x_ * 4 + (y_ % 2) * 2 + c_, "dev": z_ * 2 + y_ // 2}
 
-    z_peers = [at(x, y, (z + k) % 16, c) for k in range(1, 16)]
+    z_peers = {k: at(x, y, (z + k) % 16, c) for k in range(1, 16)}
     y_peers = [at(x, (y + k) % 4, z, c) for k in range(1, 4)]
     x_peers = [at((x + k) % 4, y, z, c) for k in range(1, 4)]
     partner = at(x, y, z, 1 - c)
 
     barrier = pltpu.get_barrier_semaphore()
-    everyone = z_peers + y_peers + x_peers + [partner]
+    near = (4, 12, 3, 13, 2, 14, 1, 15)
+    everyone = [z_peers[k] for k in near] + y_peers + x_peers + [partner]
     for peer in everyone:
         pl.semaphore_signal(barrier, inc=1, device_id=peer, device_id_type=MESH)
 
-    v_copy = pltpu.make_async_copy(v_hbm, v_vm, v_sem)
-    v_copy.start()
+    fetch = [
+        pltpu.make_async_copy(src, dst, in_sem.at[n])
+        for n, (src, dst) in enumerate(
+            ((q_hbm, q_ref), (p_hbm, p_ref), (id_hbm, id_ref), (v_hbm, v_vm))
+        )
+    ]
+    for copy in fetch:
+        copy.start()
+    for ref in (crecv,):
+        ref[...] = jnp.full(ref.shape, NEG, F32)
+    for s in range(4):
+        xrecv[s * 128 + SENT : s * 128 + 128, :] = jnp.full((128 - SENT, 128), NEG, F32)
+    fetch[0].wait()
+    fetch[1].wait()
 
     zbuf[z, 12:16, :] = jnp.zeros((4, 128), jnp.bfloat16)
     for i in range(6):
         zbuf[z, 2 * i : 2 * i + 2, :] = q_ref[:, 128 * i : 128 * i + 128]
     lists = p_ref[...]
-    zbuf[z, 12:14, 0:16] = (lists // 32).astype(F32).astype(jnp.bfloat16)
-    zbuf[z, 12:14, 16:32] = (lists % 32).astype(F32).astype(jnp.bfloat16)
-    for ref in (crecv, ):
-        ref[...] = jnp.full(ref.shape, NEG, F32)
-    for s in range(4):
-        xrecv[s * 128 + SENT : s * 128 + 128, :] = jnp.full((128 - SENT, 128), NEG, F32)
-
+    zbuf[z, 12:14, 0:16] = lax.shift_right_logical(lists, 5).astype(F32).astype(jnp.bfloat16)
+    zbuf[z, 12:14, 16:32] = (lists & 31).astype(F32).astype(jnp.bfloat16)
     pl.semaphore_wait(barrier, len(everyone))
 
     def remote(src, dst, send, recv, peer):
@@ -111,16 +119,27 @@
         return copy
 
     sent = []
-    z_copies = [
-        remote(zbuf.at[z], zbuf.at[z], zs.at[k], zr.at[k], z_peers[k]) for k in range(15)
-    ]
-    sent += z_copies
+    z_copies = {}
+
+    def z_send(block, k, n):
+        ref = zbuf.at[(z + 16 + block) % 16]
+        z_copies[n] = remote(ref, ref, zs.at[n], zr.at[n], z_peers[k])
+
+    for k in near:
+        z_send(0, k, k if k < 8 else k - 1)
     r = lax.broadcasted_iota(jnp.int32, (224, 256), 0)
     k_ = lax.broadcasted_iota(jnp.int32, (224, 256), 1)
     pick = k_ == ((r % 32) // 2) * 16 + (r // 32) * 2 + r % 2
     pick = jnp.where(pick, 1.0, 0.0).astype(jnp.bfloat16)
-    for copy in z_copies:
-        copy.wait_recv()
+    for j in (1, 2, 3, 4):
+        z_copies[j].wait_recv()
+        z_send(-j, 4, 15 + j)
+        z_copies[15 - j].wait_recv()
+        if j < 4:
+            z_send(j, 12, 19 + j)
+    sent += list(z_copies.values())
+    for n in range(16, 23):
+        z_copies[n].wait_recv()
     rows = jnp.dot(pick, zbuf[...].reshape(256, 128), preferred_element_type=F32)
     rows = rows.astype(jnp.bfloat16)
     for h in range(2):
@@ -166,27 +185,28 @@
                 second[h, b1, b2 - 1].wait_recv()
                 forward_core(h, b1, b2)
     sent += list(first.values()) + list(second.values()) + list(cross.values())
+    fetch[2].wait()
+    fetch[3].wait()
+
+    def score(core):
+        @pl.loop(0, 2)
+        def _(half):
+            block = gath[core, pl.ds(half * 2, 2)].reshape(256, 896)
+            turned = block[:, 768:896].astype(F32).T[:32, :].astype(jnp.int32)
+            scores = lax.dot_general(
+                v_vm[...], block[:, :768], (((1,), (1,)), ((), ())), preferred_element_type=F32
+            )
+            for t in range(2):
+                s = core * 4 + half * 2 + t
+                codes[pl.ds(pl.multiple_of(32 * s, 32), 32), :] = turned[:, 128 * t : 128 * t + 128]
+                for j in range(64):
+                    row = pl.multiple_of(j * 64 + s * 8, 8)
+                    prod[pl.ds(row, 8), :] = scores[8 * j : 8 * j + 8, 128 * t : 128 * t + 128]
+
+    score(c)
     for copy in cross.values():
         copy.wait_recv()
-    v_copy.wait()
-
-    for s in range(8):
-        part = gath[s // 4, s % 4].reshape(128, 896)[:, 768:896]
-        turned = part.astype(F32).T
-        codes[32 * s : 32 * s + 32, :] = turned[:32, :].astype(jnp.int32)
-
-    @pl.loop(0, 4)
-    def _(s2):
-        block = gath[s2 // 2, pl.ds((s2 % 2) * 2, 2)].reshape(256, 896)[:, :768]
-        for m in range(4):
-            scores = lax.dot_general(
-                v_vm[128 * m : 128 * m + 128, :], block,
-                (((1,), (1,)), ((), ())), preferred_element_type=F32,
-            )
-            for j in range(16):
-                for t in range(2):
-                    row = pl.multiple_of((16 * m + j) * 64 + (s2 * 2 + t) * 8, 8)
-                    prod[pl.ds(row, 8), :] = scores[8 * j : 8 * j + 8, 128 * t : 128 * t + 128]
+    score(1 - c)
 
     high = [codes[pl.ds(p, 8, stride=32), :] for p in range(16)]
     bits = [jnp.left_shift(jnp.int32(1), codes[pl.ds(16 + p, 8, stride=32), :]) for p in range(16)]
@@ -204,8 +224,8 @@
         for i in range(32):
             value = prod[pl.ds(g * 256 + (i // 8) * 64 + i % 8, 8, stride=8), :]
             which = id_ref[g * 32 + i]
-            word = words[which // 32]
-            keep = (word & jnp.left_shift(jnp.int32(1), which % 32)) != 0
+            word = words[lax.shift_right_logical(which, 5)]
+            keep = (word & jnp.left_shift(jnp.int32(1), which & 31)) != 0
             xs.append(jnp.where(keep, value, NEG))
         xs = sort_desc(xs)
         for i in range(32):
@@ -331,7 +351,7 @@
     for s in range(16):
         zsend[s] = turned[2 * s : 2 * s + 2, :]
     copies = [
-        remote(zsend.at[(z + k + 1) % 16], zrecv.at[z], rzs.at[k], rzr.at[k], z_peers[k])
+        remote(zsend.at[(z + k + 1) % 16], zrecv.at[z], rzs.at[k], rzr.at[k], z_peers[k + 1])
         for k in range(15)
     ]
     sent += copies
@@ -356,11 +376,12 @@
     return pl.pallas_call(
         kernel,
         out_shape=jax.ShapeDtypeStruct((2, K), F32),
-        in_specs=[
-            vmem, vmem, pl.BlockSpec(memory_space=pl.ANY), pl.BlockSpec(memory_space=pltpu.SMEM),
-        ],
+        in_specs=[pl.BlockSpec(memory_space=pl.ANY)] * 4,
         out_specs=vmem,
         scratch_shapes=[
+            pltpu.VMEM((2, 768), jnp.bfloat16),
+            pltpu.VMEM((2, 16), jnp.int32),
+            pltpu.SMEM((512,), jnp.int32),
             pltpu.VMEM((16, 16, 128), jnp.bfloat16),
             pltpu.VMEM((2, 4, 4, 2, 16, 896), jnp.bfloat16),
             pltpu.VMEM((512, 768), jnp.bfloat16),
@@ -383,11 +404,11 @@
             pltpu.VMEM((128, 128), F32),
             pltpu.VMEM((16, 2, 128), F32),
             pltpu.VMEM((16, 2, 128), F32),
-            dma, dma((15,)), dma((15,)), dma((2, 3)), dma((2, 3)), dma((2, 4, 3)), dma((2, 4, 3)),
+            dma((4,)), dma((23,)), dma((23,)), dma((2, 3)), dma((2, 3)), dma((2, 4, 3)), dma((2, 4, 3)),
             dma((2, 16)), dma((2, 16)), dma((1,)), dma((1,)), dma((3,)), dma((3,)),
             dma((3,)), dma((3,)), dma((15,)), dma((15,)),
         ],
-        compiler_params=pltpu.CompilerParams(collective_id=0, has_side_effects=True),
+        compiler_params=pltpu.CompilerParams(collective_id=0, has_side_effects=True, vmem_limit_bytes=32 * 2**20),
     )(queries, probes, vectors, list_ids)
 
 

time: 68.5 us -> 64.6 us (0.943)
  the two profiles are of different devices: /device:TPU:8 before, /device:TPU:32 now
where the time goes in v2:
time: 64.6 us; the launch traced here: 64.3 us
  Pallas kernels  60.6 us (94%)
  local copies, waits for them, and re-layouts  3.74 us (6%)
    pallas_call x1, Pallas kernels, local(): pl.pallas_call(kernel, out_shape=jax.ShapeDtypeStruct((2, K), F32), in_sp...  60.6 us
    unnamed x9, local copies, waits for them, and re-layouts  3.74 us

profile of v2, /device:TPU:32, one launch (start us, length us, event | category | flops | bytes accessed | tf_op | source)
XLA Modules:
  0.0 64.3 jit_solution(2628377327808775263)
XLA Ops:
  0.0 0.0 copy-start
  0.0 1.1 %copy-done = bf16[512,768]{1,0:T(8,128)(2,1)S(1)} copy-done((bf16[512,768]{1,0:T(8,128)(2,1)S(1)}, bf16[512,768]{1,0:T(8,128)(2,1)}, u32[]{:S(2)}) %copy-start) | copy-done | bytes 786456
  1.1 0.0 copy-start.1
  1.1 0.7 %copy-done.1 = bf16[2,768]{1,0:T(2,128)(2,1)S(1)} copy-done((bf16[2,768]{1,0:T(2,128)(2,1)S(1)}, bf16[2,768]{1,0:T(2,128)(2,1)}, u32[]{:S(2)}) %copy-start.1) | copy-done | bytes 3096
  1.8 0.0 copy-start.2
  1.8 0.7 %copy-done.2 = s32[512]{0:T(512)S(1)} copy-done((s32[512]{0:T(512)S(1)}, s32[512]{0:T(512)}, u32[]{:S(2)}) %copy-start.2) | copy-done | bytes 2072
  2.5 0.0 copy-start.3
  2.5 0.7 %copy-done.3 = s32[2,16]{1,0:T(2,128)S(1)} copy-done((s32[2,16]{1,0:T(2,128)S(1)}, s32[2,16]{1,0:T(2,128)}, u32[]{:S(2)}) %copy-start.3) | copy-done | bytes 152
  3.2 60.6 %shard_map.46 = f32[2,100]{1,0:T(2,128)S(1)} custom-call(bf16[2,768]{1,0:T(2,128)(2,1)S(1)} %copy-done.1, s32[2,16]{1,0:T(2,128)S(1)} %copy-done.3, bf16[512,768]{1,0:T(8,128)(2,1)S(1)} %copy-done, s32[512]{0:T(512)S(1)} %copy-done.2), custom_call_target="tpu_custom_call" | custom-call | tf_op jit(solution)/shard_map/pallas_call | solution.py:376
  63.8 0.6 copy.6
Async XLA Ops:
  0.0 1.1 %copy-start = (bf16[512,768]{1,0:T(8,128)(2,1)S(1)}, bf16[512,768]{1,0:T(8,128)(2,1)}, u32[]{:S(2)}) copy-start(bf16[512,768]{1,0:T(8,128)(2,1)} %v_hbm.1) | copy-start | bytes 2359300
  1.1 0.7 %copy-start.1 = (bf16[2,768]{1,0:T(2,128)(2,1)S(1)}, bf16[2,768]{1,0:T(2,128)(2,1)}, u32[]{:S(2)}) copy-start(bf16[2,768]{1,0:T(2,128)(2,1)} %q_hbm.1) | copy-start | bytes 9220
  1.8 0.7 %copy-start.2 = (s32[512]{0:T(512)S(1)}, s32[512]{0:T(512)}, u32[]{:S(2)}) copy-start(s32[512]{0:T(512)} %id_hbm.1) | copy-start | bytes 6148
  2.5 0.7 %copy-start.3 = (s32[2,16]{1,0:T(2,128)S(1)}, s32[2,16]{1,0:T(2,128)}, u32[]{:S(2)}) copy-start(s32[2,16]{1,0:T(2,128)} %p_hbm.1) | copy-start | bytes 388

commit v3 on v2

--- a/solution.py
+++ b/solution.py
@@ -12,6 +12,9 @@
 NEG = -1.0e30
 MESH = pl.DeviceIdType.MESH
 F32 = jnp.float32
+
+
+SLOT = {k % 16: n for n, k in enumerate((0, 1, 2, 3, 4, -1, -2, -3, 5, 6, 7, 8, -4, -5, -6, -7))}
 
 
 def exchange(a, b):
@@ -64,9 +67,9 @@
 
 def kernel(
     q_hbm, p_hbm, v_hbm, id_hbm, o_ref,
-    q_ref, p_ref, id_ref, zbuf, gath, v_vm, prod, words, codes, runs, runs2, csend, crecv, ctmp,
-    xsend, xrecv, atmp, apair, row_a, row_b, row_c, ysend, yrecv, zsend, zrecv,
-    in_sem, zs, zr, fs, fr, ss, sr, cs, cr, rcs, rcr, rxs, rxr, rys, ryr, rzs, rzr,
+    q_ref, p_ref, id_ref, zbuf, ga, gb, gc, v_vm, prod, words, codes, runs, runs2, csend, crecv, ctmp,
+    xsend, xrecv, atmp, apair, row_a, row_b, row_c, dsend, drecv,
+    in_sem, done, zs, zr, fs, fr, ss, sr, cs, cr, rcs, rcr, rxs, rxr, rds, rdr,
 ):
     pb, dev = lax.axis_index("pb"), lax.axis_index("dev")
     x, ylo, c = pb // 4, (pb // 2) % 2, pb % 2
@@ -102,12 +105,12 @@
     fetch[0].wait()
     fetch[1].wait()
 
-    zbuf[z, 12:16, :] = jnp.zeros((4, 128), jnp.bfloat16)
+    zbuf[0, 12:16, :] = jnp.zeros((4, 128), jnp.bfloat16)
     for i in range(6):
-        zbuf[z, 2 * i : 2 * i + 2, :] = q_ref[:, 128 * i : 128 * i + 128]
+        zbuf[0, 2 * i : 2 * i + 2, :] = q_ref[:, 128 * i : 128 * i + 128]
     lists = p_ref[...]
-    zbuf[z, 12:14, 0:16] = lax.shift_right_logical(lists, 5).astype(F32).astype(jnp.bfloat16)
-    zbuf[z, 12:14, 16:32] = (lists & 31).astype(F32).astype(jnp.bfloat16)
+    zbuf[0, 12:14, 0:16] = lax.shift_right_logical(lists, 5).astype(F32).astype(jnp.bfloat16)
+    zbuf[0, 12:14, 16:32] = (lists & 31).astype(F32).astype(jnp.bfloat16)
     pl.semaphore_wait(barrier, len(everyone))
 
     def remote(src, dst, send, recv, peer):
@@ -118,94 +121,130 @@
         copy.start()
         return copy
 
-    sent = []
-    z_copies = {}
+    def take(ref, recv):
+        pltpu.make_async_remote_copy(
+            src_ref=ref, dst_ref=ref, send_sem=done.at[0], recv_sem=recv,
+            device_id=partner, device_id_type=MESH,
+        ).wait_recv()
+
+    def drain(ref, send):
+        pltpu.make_async_remote_copy(
+            src_ref=ref, dst_ref=ref, send_sem=send, recv_sem=done.at[0],
+            device_id=partner, device_id_type=MESH,
+        ).wait_send()
 
     def z_send(block, k, n):
-        ref = zbuf.at[(z + 16 + block) % 16]
-        z_copies[n] = remote(ref, ref, zs.at[n], zr.at[n], z_peers[k])
+        remote(zbuf.at[SLOT[block % 16]], zbuf.at[SLOT[(block - k) % 16]], zs.at[0], zr.at[n], z_peers[k])
 
     for k in near:
-        z_send(0, k, k if k < 8 else k - 1)
-    r = lax.broadcasted_iota(jnp.int32, (224, 256), 0)
-    k_ = lax.broadcasted_iota(jnp.int32, (224, 256), 1)
-    pick = k_ == ((r % 32) // 2) * 16 + (r // 32) * 2 + r % 2
+        z_send(0, k, min(k, 16 - k))
+    r = lax.broadcasted_iota(jnp.int32, (112, 128), 0)
+    k_ = lax.broadcasted_iota(jnp.int32, (112, 128), 1)
+    pick = k_ == lax.shift_right_logical(r & 15, 1) * 16 + lax.shift_right_logical(r, 4) * 2 + (r & 1)
     pick = jnp.where(pick, 1.0, 0.0).astype(jnp.bfloat16)
+
+    def place(h):
+        rows = jnp.dot(
+            pick, zbuf[8 * h : 8 * h + 8].reshape(128, 128), preferred_element_type=F32
+        )
+        for i in range(3):
+            ga[c, h, x, y, :, 128 * i : 128 * i + 128] = rows[16 * i : 16 * i + 16, :].astype(jnp.bfloat16)
+            gb[c, h, y, x, :, 128 * i : 128 * i + 128] = rows[16 * i + 48 : 16 * i + 64, :].astype(jnp.bfloat16)
+        return rows[96:112, :]
+
+    kinds = [
+        (lambda a2, h=h, g=g: g.at[c, h, a2], *axes)
+        for h in range(2)
+        for g, axes in ((ga, (x, y, y_peers, x_peers)), (gb, (y, x, x_peers, y_peers)))
+    ]
+    whole = [ga.at[:, 0], gb.at[:, 0], ga.at[:, 1], gb.at[:, 1], gc]
+    kinds.append((lambda a2: gc.at[c, a2], x, y, y_peers, x_peers))
+
+    def send_first(n):
+        group, a2, a1, peers, _ = kinds[n]
+        ref = group(a2).at[a1]
+        for k in (1, 0, 2):
+            remote(ref, ref, fs.at[n], fr.at[n, k], peers[k])
+
+    def send_second(n, b):
+        group, a2, a1, _, peers = kinds[n]
+        ref = group(a2).at[(a1 + 4 - b) % 4]
+        for k in (1, 0, 2):
+            remote(ref, ref, ss.at[n], sr.at[n, k], peers[k])
+
+    def send_cross(n, b):
+        ref = kinds[n][0]((kinds[n][1] + 4 - b) % 4)
+        remote(ref, ref, cs.at[n], cr.at[n], partner)
+
+    def pass_first(which):
+        for b in (1, 3, 2):
+            for n in which:
+                take(kinds[n][0](kinds[n][1]).at[0], fr.at[n, b - 1])
+                send_second(n, b)
+        for n in which:
+            send_cross(n, 0)
+
+    def pass_second(which):
+        for b in (1, 3, 2):
+            for n in which:
+                take(kinds[n][0](kinds[n][1]), sr.at[n, b - 1])
+                send_cross(n, b)
+
+    def start(which):
+        for n in which:
+            send_first(n)
+        for n in which:
+            send_second(n, 0)
+
     for j in (1, 2, 3, 4):
-        z_copies[j].wait_recv()
-        z_send(-j, 4, 15 + j)
-        z_copies[15 - j].wait_recv()
+        take(zbuf.at[0:2], zr.at[j])
+        z_send(-j, 4, 0)
         if j < 4:
-            z_send(j, 12, 19 + j)
-    sent += list(z_copies.values())
-    for n in range(16, 23):
-        z_copies[n].wait_recv()
-    rows = jnp.dot(pick, zbuf[...].reshape(256, 128), preferred_element_type=F32)
-    rows = rows.astype(jnp.bfloat16)
-    for h in range(2):
-        for i in range(7):
-            gath[c, x, y, h, :, 128 * i : 128 * i + 128] = rows[
-                32 * i + 16 * h : 32 * i + 16 * h + 16, :
-            ]
-
-    def piece(h, back1, back2):
-        if h == 0:
-            return gath.at[c, (x + 4 - back2) % 4, (y + 4 - back1) % 4, h]
-        return gath.at[c, (x + 4 - back1) % 4, (y + 4 - back2) % 4, h]
-
-    peers1 = [y_peers, x_peers]
-    peers2 = [x_peers, y_peers]
-    first, second, cross = {}, {}, {}
-    for k in range(3):
-        for h in range(2):
-            ref = piece(h, 0, 0)
-            first[h, k] = remote(ref, ref, fs.at[h, k], fr.at[h, k], peers1[h][k])
-
-    def forward2(h, b):
-        ref = piece(h, b, 0)
-        for k in range(3):
-            second[h, b, k] = remote(ref, ref, ss.at[h, b, k], sr.at[h, b, k], peers2[h][k])
-
-    def forward_core(h, b1, b2):
-        ref, n = piece(h, b1, b2), b1 * 4 + b2
-        cross[h, b1, b2] = remote(ref, ref, cs.at[h, n], cr.at[h, n], partner)
-
-    for h in range(2):
-        forward2(h, 0)
-    for h in range(2):
-        forward_core(h, 0, 0)
-    for b in (1, 3, 2):
-        for h in range(2):
-            first[h, b - 1].wait_recv()
-            forward2(h, b)
-            forward_core(h, b, 0)
-    for b1 in (0, 1, 3, 2):
-        for b2 in (1, 3, 2):
-            for h in range(2):
-                second[h, b1, b2 - 1].wait_recv()
-                forward_core(h, b1, b2)
-    sent += list(first.values()) + list(second.values()) + list(cross.values())
+            z_send(j, 12, 0)
+    near_codes = place(0)
+    start((0, 1))
+    take(zbuf.at[0:7], zr.at[0])
+    far_codes = place(1)
+    gc[c, x, y] = (near_codes + pltpu.roll(far_codes, 32, axis=1)).astype(jnp.bfloat16)
+    start((2, 3, 4))
+    pass_first((0, 1))
+    pass_first((2, 3, 4))
+    pass_second((0, 1))
+    pass_second((2, 3, 4))
+
     fetch[2].wait()
     fetch[3].wait()
 
     def score(core):
         @pl.loop(0, 2)
         def _(half):
-            block = gath[core, pl.ds(half * 2, 2)].reshape(256, 896)
-            turned = block[:, 768:896].astype(F32).T[:32, :].astype(jnp.int32)
+            block = jnp.concatenate(
+                [
+                    jnp.concatenate(
+                        [ga[core, h, half * 2 + t].reshape(64, 384), gb[core, h, :, half * 2 + t].reshape(64, 384)],
+                        axis=1,
+                    )
+                    for t in range(2)
+                    for h in range(2)
+                ],
+                axis=0,
+            )
             scores = lax.dot_general(
-                v_vm[...], block[:, :768], (((1,), (1,)), ((), ())), preferred_element_type=F32
+                v_vm[...], block, (((1,), (1,)), ((), ())), preferred_element_type=F32
             )
             for t in range(2):
                 s = core * 4 + half * 2 + t
-                codes[pl.ds(pl.multiple_of(32 * s, 32), 32), :] = turned[:, 128 * t : 128 * t + 128]
+                turned = gc[core, half * 2 + t].reshape(64, 128).astype(F32).T.astype(jnp.int32)
+                codes[pl.ds(pl.multiple_of(32 * s, 32), 32), :] = jnp.concatenate(
+                    [turned[0:32, :], turned[32:64, :]], axis=1
+                )
                 for j in range(64):
                     row = pl.multiple_of(j * 64 + s * 8, 8)
                     prod[pl.ds(row, 8), :] = scores[8 * j : 8 * j + 8, 128 * t : 128 * t + 128]
 
     score(c)
-    for copy in cross.values():
-        copy.wait_recv()
+    for n in range(5):
+        take(whole[n].at[1 - c], cr.at[n])
     score(1 - c)
 
     high = [codes[pl.ds(p, 8, stride=32), :] for p in range(16)]
@@ -279,11 +318,8 @@
 
     merge_top(run_load(runs2, 0), run_load(runs2, 256), run_load(runs, 0), run_store(runs, 0), split_store)
 
-    copy = remote(
-        csend.at[1 - c, pl.ds(0, SENT)], crecv.at[pl.ds(0, SENT)], rcs.at[0], rcr.at[0], partner
-    )
-    sent.append(copy)
-    copy.wait_recv()
+    remote(csend.at[1 - c, pl.ds(0, SENT)], crecv.at[pl.ds(0, SENT)], rcs.at[0], rcr.at[0], partner)
+    take(crecv.at[pl.ds(0, SENT)], rcr.at[0])
 
     def x_store(i, value):
         xsend[pl.ds(i, 4, stride=128), :] = value
@@ -293,17 +329,13 @@
     def x_rows(s):
         return pl.ds(pl.multiple_of(s * 128, 128), SENT)
 
-    copies = [
+    for k in (1, 0, 2):
         remote(
             xsend.at[x_rows((x + k + 1) % 4)], xrecv.at[x_rows(x)],
-            rxs.at[k], rxr.at[k], x_peers[k],
+            rxs.at[0], rxr.at[0], x_peers[k],
         )
-        for k in range(3)
-    ]
-    sent += copies
     xrecv[x_rows(x), :] = xsend[x_rows(x), :]
-    for copy in copies:
-        copy.wait_recv()
+    take(xrecv.at[pl.ds(0, 3 * SENT)], rxr.at[0])
 
     def pair_store(i, value):
         apair[pl.ds(i, 2, stride=128), :] = value
@@ -327,47 +359,39 @@
         row_b[...] = pltpu.roll(row_a[...], 128 - distance, axis=1)
         merge_top(row_load(row_a), row_load(row_b), row_load(row_c), row_store(row_c), row_store(row_a))
 
-    ysend[...] = row_a[...].T
-
-    def y_rows(s):
-        return pl.ds(pl.multiple_of(s * 32, 32), 32)
-
-    copies = [
-        remote(
-            ysend.at[y_rows((y + k + 1) % 4)], yrecv.at[y_rows(y)],
-            rys.at[k], ryr.at[k], y_peers[k],
-        )
-        for k in range(3)
-    ]
-    sent += copies
-    yrecv[y_rows(y), :] = ysend[y_rows(y), :]
-    for copy in copies:
-        copy.wait_recv()
-    row_a[...] = yrecv[...].T
-    fold_lanes(64)
-    fold_lanes(32)
-
     turned = row_a[...].T
-    for s in range(16):
-        zsend[s] = turned[2 * s : 2 * s + 2, :]
-    copies = [
-        remote(zsend.at[(z + k + 1) % 16], zrecv.at[z], rzs.at[k], rzr.at[k], z_peers[k + 1])
-        for k in range(15)
-    ]
-    sent += copies
-    zrecv[z] = zsend[z]
-    for copy in copies:
-        copy.wait_recv()
-    row_b[32:128, :] = jnp.full((96, 128), NEG, F32)
-    for s in range(16):
-        row_b[2 * s : 2 * s + 2, :] = zrecv[s]
+    for h in range(2):
+        for y_ in range(4):
+            for r8 in range(8):
+                row = h * 64 + y_ * 16 + r8 * 2
+                dsend[y_ * 16 + h * 8 + r8] = turned[row : row + 2, :]
+    for k in (8, 7, 9, 6, 10, 5, 11, 4, 12, 3, 13, 2, 14, 1, 15, 0):
+        for j in (2, 1, 3, 0):
+            if (j, k) == (0, 0):
+                continue
+            n = j * 16 + SLOT[k]
+            remote(
+                dsend.at[((y + j) % 4) * 16 + SLOT[k]], drecv.at[n], rds.at[0], rdr.at[0],
+                at(x, (y + j) % 4, (z + k) % 16, c),
+            )
+    drecv[0] = dsend[y * 16]
+    take(drecv.at[1:64], rdr.at[0])
+    for n in range(64):
+        row_b[2 * n : 2 * n + 2, :] = drecv[n]
     row_a[...] = row_b[...].T
-    for distance in (16, 8, 4, 2):
+    for distance in (64, 32, 16, 8, 4, 2):
         fold_lanes(distance)
     o_ref[...] = row_a[...].T[0:2, 0:K]
 
-    for copy in sent:
-        copy.wait_send()
+    drain(zbuf.at[0:15], zs.at[0])
+    for n in range(5):
+        group, a2 = kinds[n][0], kinds[n][1]
+        drain(group(a2).at[0:3], fs.at[n])
+        drain(whole[n].at[c, 0:3], ss.at[n])
+        drain(whole[n].at[c], cs.at[n])
+    drain(crecv.at[pl.ds(0, SENT)], rcs.at[0])
+    drain(xrecv.at[pl.ds(0, 3 * SENT)], rxs.at[0])
+    drain(dsend.at[0:63], rds.at[0])
 
 
 def local(queries, probes, vectors, list_ids):
@@ -376,14 +400,16 @@
     return pl.pallas_call(
         kernel,
         out_shape=jax.ShapeDtypeStruct((2, K), F32),
-        in_specs=[pl.BlockSpec(memory_space=pl.ANY)] * 4,
+        in_specs=[pl.BlockSpec(memory_space=pltpu.HBM)] * 4,
         out_specs=vmem,
         scratch_shapes=[
             pltpu.VMEM((2, 768), jnp.bfloat16),
             pltpu.VMEM((2, 16), jnp.int32),
             pltpu.SMEM((512,), jnp.int32),
             pltpu.VMEM((16, 16, 128), jnp.bfloat16),
-            pltpu.VMEM((2, 4, 4, 2, 16, 896), jnp.bfloat16),
+            pltpu.VMEM((2, 2, 4, 4, 16, 384), jnp.bfloat16),
+            pltpu.VMEM((2, 2, 4, 4, 16, 384), jnp.bfloat16),
+            pltpu.VMEM((2, 4, 4, 16, 128), jnp.bfloat16),
             pltpu.VMEM((512, 768), jnp.bfloat16),
             pltpu.VMEM((4096, 128), F32),
             pltpu.VMEM((32, 8, 128), jnp.int32),
@@ -400,15 +426,12 @@
             pltpu.VMEM((128, 128), F32),
             pltpu.VMEM((128, 128), F32),
             pltpu.VMEM((128, 128), F32),
-            pltpu.VMEM((128, 128), F32),
-            pltpu.VMEM((128, 128), F32),
-            pltpu.VMEM((16, 2, 128), F32),
-            pltpu.VMEM((16, 2, 128), F32),
-            dma((4,)), dma((23,)), dma((23,)), dma((2, 3)), dma((2, 3)), dma((2, 4, 3)), dma((2, 4, 3)),
-            dma((2, 16)), dma((2, 16)), dma((1,)), dma((1,)), dma((3,)), dma((3,)),
-            dma((3,)), dma((3,)), dma((15,)), dma((15,)),
+            pltpu.VMEM((64, 2, 128), F32),
+            pltpu.VMEM((64, 2, 128), F32),
+            dma((4,)), dma((1,)), dma((1,)), dma((5,)), dma((5,)), dma((5, 3)), dma((5,)), dma((5, 3)),
+            dma((5,)), dma((5,)), dma((1,)), dma((1,)), dma((1,)), dma((1,)), dma((1,)), dma((1,)),
         ],
-        compiler_params=pltpu.CompilerParams(collective_id=0, has_side_effects=True, vmem_limit_bytes=32 * 2**20),
+        compiler_params=pltpu.CompilerParams(collective_id=0, has_side_effects=True),
     )(queries, probes, vectors, list_ids)
 
 

time: 64.6 us -> 57 us (0.88)
  the two profiles are of different devices: /device:TPU:32 before, /device:TPU:1 now
where the time goes in v3:
time: 57 us; the launch traced here: 56.9 us
  Pallas kernels  55.6 us (98%)
  local copies, waits for them, and re-layouts  1.24 us (2%)
    pallas_call x1, Pallas kernels, local(): pl.pallas_call(kernel, out_shape=jax.ShapeDtypeStruct((2, K), F32), in_sp...  55.6 us
    unnamed x1, local copies, waits for them, and re-layouts  1.24 us

profile of v3, /device:TPU:1, one launch (start us, length us, event | category | flops | bytes accessed | tf_op | source)
XLA Modules:
  0.0 56.9 jit_solution(13972637031739480189)
XLA Ops:
  0.0 55.6 %shard_map.46 = f32[2,100]{1,0:T(2,128)} custom-call(bf16[2,768]{1,0:T(2,128)(2,1)} %q_hbm.1, s32[2,16]{1,0:T(2,128)} %p_hbm.1, bf16[512,768]{1,0:T(8,128)(2,1)} %v_hbm.1, s32[512]{0:T(512)} %id_hbm.1), custom_call_target="tpu_custom_call" | custom-call | tf_op jit(solution)/shard_map/pallas_call | solution.py:400
  55.6 1.2 %copy.6 = f32[2,100]{1,0:T(2,128)} copy(f32[2,100]{1,0:T(2,128)} %shard_map.46) | data formatting | bytes 1600

commit v4 on v3

--- a/solution.py
+++ b/solution.py
@@ -45,6 +45,38 @@
     return xs
 
 
+def clean_rows(xs, up=None):
+    def order(hi, lo):
+        if up is None:
+            return hi, lo
+        if up is True:
+            return lo, hi
+        return jnp.where(up, lo, hi), jnp.where(up, hi, lo)
+
+    xs = list(xs)
+    for d in (8, 4, 2, 1):
+        for i in range(16):
+            if i & d == 0:
+                xs[i], xs[i + d] = order(*exchange(xs[i], xs[i + d]))
+    row = lax.broadcasted_iota(jnp.int32, (8, 128), 0)
+    for d in (4, 2, 1):
+        lower = (row & d) == 0
+        if up is None:
+            larger = lower
+        elif up is True:
+            larger = (row & d) != 0
+        else:
+            larger = lower != up
+        for i in range(16):
+            if d == 4:
+                other = pltpu.roll(xs[i], 4, axis=0)
+            else:
+                other = jnp.where(lower, pltpu.roll(xs[i], 8 - d, axis=0), pltpu.roll(xs[i], d, axis=0))
+            hi, lo = exchange(xs[i], other)
+            xs[i] = jnp.where(larger, hi, lo)
+    return xs
+
+
 def merge_top(load_a, load_b, tmp_load, tmp_store, store):
     @pl.loop(0, 8)
     def _(g):
@@ -67,9 +99,9 @@
 
 def kernel(
     q_hbm, p_hbm, v_hbm, id_hbm, o_ref,
-    q_ref, p_ref, id_ref, zbuf, ga, gb, gc, v_vm, prod, words, codes, runs, runs2, csend, crecv, ctmp,
-    xsend, xrecv, atmp, apair, row_a, row_b, row_c, dsend, drecv,
-    in_sem, done, zs, zr, fs, fr, ss, sr, cs, cr, rcs, rcr, rxs, rxr, rds, rdr,
+    q_ref, p_ref, ids, row_of, bit_of, rows1, bits1, rows2, bits2, zbuf, ga, gb, gc, v_vm, prod, words, words2, codes, runs, runs2, ctmp,
+    xsend, xrecv, row_a, row_b, dsend, drecv,
+    in_sem, done, vs, vr, zs, zr, fs, fr, ss, sr, rxs, rxr, rds, rdr,
 ):
     pb, dev = lax.axis_index("pb"), lax.axis_index("dev")
     x, ylo, c = pb // 4, (pb // 2) % 2, pb % 2
@@ -93,15 +125,14 @@
     fetch = [
         pltpu.make_async_copy(src, dst, in_sem.at[n])
         for n, (src, dst) in enumerate(
-            ((q_hbm, q_ref), (p_hbm, p_ref), (id_hbm, id_ref), (v_hbm, v_vm))
+            ((q_hbm, q_ref), (p_hbm, p_ref), (id_hbm, ids), (v_hbm, v_vm.at[0]))
         )
     ]
     for copy in fetch:
         copy.start()
-    for ref in (crecv,):
-        ref[...] = jnp.full(ref.shape, NEG, F32)
     for s in range(4):
-        xrecv[s * 128 + SENT : s * 128 + 128, :] = jnp.full((128 - SENT, 128), NEG, F32)
+        pad = s * 128 + (0 if s % 2 else SENT)
+        xrecv[pad : pad + 128 - SENT, :] = jnp.full((128 - SENT, 128), NEG, F32)
     fetch[0].wait()
     fetch[1].wait()
 
@@ -138,6 +169,17 @@
 
     for k in near:
         z_send(0, k, min(k, 16 - k))
+    remote(v_hbm, v_vm.at[1], vs.at[0], vr.at[0], partner)
+    fetch[2].wait()
+    row_of[...] = lax.shift_right_logical(ids[...], 5)
+    bit_of[...] = jnp.left_shift(jnp.int32(1), ids[...] & 31)
+    tables = [
+        pltpu.make_async_copy(row_of, rows1, in_sem.at[4]), pltpu.make_async_copy(bit_of, bits1, in_sem.at[5])
+    ]
+    for copy in tables:
+        copy.start()
+    remote(row_of, rows2, vs.at[1], vr.at[1], partner)
+    remote(bit_of, bits2, vs.at[2], vr.at[2], partner)
     r = lax.broadcasted_iota(jnp.int32, (112, 128), 0)
     k_ = lax.broadcasted_iota(jnp.int32, (112, 128), 1)
     pick = k_ == lax.shift_right_logical(r & 15, 1) * 16 + lax.shift_right_logical(r, 4) * 2 + (r & 1)
@@ -148,17 +190,17 @@
             pick, zbuf[8 * h : 8 * h + 8].reshape(128, 128), preferred_element_type=F32
         )
         for i in range(3):
-            ga[c, h, x, y, :, 128 * i : 128 * i + 128] = rows[16 * i : 16 * i + 16, :].astype(jnp.bfloat16)
-            gb[c, h, y, x, :, 128 * i : 128 * i + 128] = rows[16 * i + 48 : 16 * i + 64, :].astype(jnp.bfloat16)
+            ga[h, x, y, :, 128 * i : 128 * i + 128] = rows[16 * i : 16 * i + 16, :].astype(jnp.bfloat16)
+            gb[h, y, x, :, 128 * i : 128 * i + 128] = rows[16 * i + 48 : 16 * i + 64, :].astype(jnp.bfloat16)
         return rows[96:112, :]
 
     kinds = [
-        (lambda a2, h=h, g=g: g.at[c, h, a2], *axes)
+        (lambda a2, h=h, g=g: g.at[h, a2], *axes)
         for h in range(2)
         for g, axes in ((ga, (x, y, y_peers, x_peers)), (gb, (y, x, x_peers, y_peers)))
     ]
-    whole = [ga.at[:, 0], gb.at[:, 0], ga.at[:, 1], gb.at[:, 1], gc]
-    kinds.append((lambda a2: gc.at[c, a2], x, y, y_peers, x_peers))
+    whole = [ga.at[0], gb.at[0], ga.at[1], gb.at[1], gc]
+    kinds.append((lambda a2: gc.at[a2], x, y, y_peers, x_peers))
 
     def send_first(n):
         group, a2, a1, peers, _ = kinds[n]
@@ -172,23 +214,16 @@
         for k in (1, 0, 2):
             remote(ref, ref, ss.at[n], sr.at[n, k], peers[k])
 
-    def send_cross(n, b):
-        ref = kinds[n][0]((kinds[n][1] + 4 - b) % 4)
-        remote(ref, ref, cs.at[n], cr.at[n], partner)
-
     def pass_first(which):
         for b in (1, 3, 2):
             for n in which:
                 take(kinds[n][0](kinds[n][1]).at[0], fr.at[n, b - 1])
                 send_second(n, b)
-        for n in which:
-            send_cross(n, 0)
 
     def pass_second(which):
         for b in (1, 3, 2):
             for n in which:
                 take(kinds[n][0](kinds[n][1]), sr.at[n, b - 1])
-                send_cross(n, b)
 
     def start(which):
         for n in which:
@@ -205,67 +240,73 @@
     start((0, 1))
     take(zbuf.at[0:7], zr.at[0])
     far_codes = place(1)
-    gc[c, x, y] = (near_codes + pltpu.roll(far_codes, 32, axis=1)).astype(jnp.bfloat16)
-    start((2, 3, 4))
+    gc[x, y] = (near_codes + pltpu.roll(far_codes, 32, axis=1)).astype(jnp.bfloat16)
+    start((4, 2, 3))
     pass_first((0, 1))
-    pass_first((2, 3, 4))
+    pass_first((4, 2, 3))
     pass_second((0, 1))
-    pass_second((2, 3, 4))
-
-    fetch[2].wait()
     fetch[3].wait()
-
-    def score(core):
+    for copy in tables:
+        copy.wait()
+    take(v_vm.at[1], vr.at[0])
+    take(rows2, vr.at[1])
+    take(bits2, vr.at[2])
+
+    def score(h):
+        block = jnp.concatenate(
+            [
+                jnp.concatenate([ga[h, s].reshape(64, 384), gb[h, :, s].reshape(64, 384)], axis=1)
+                for s in range(4)
+            ],
+            axis=0,
+        )
+
         @pl.loop(0, 2)
-        def _(half):
-            block = jnp.concatenate(
-                [
-                    jnp.concatenate(
-                        [ga[core, h, half * 2 + t].reshape(64, 384), gb[core, h, :, half * 2 + t].reshape(64, 384)],
-                        axis=1,
-                    )
-                    for t in range(2)
-                    for h in range(2)
-                ],
-                axis=0,
+        def _(core):
+            scores = lax.dot_general(
+                v_vm[core], block, (((1,), (1,)), ((), ())), preferred_element_type=F32
             )
-            scores = lax.dot_general(
-                v_vm[...], block, (((1,), (1,)), ((), ())), preferred_element_type=F32
-            )
-            for t in range(2):
-                s = core * 4 + half * 2 + t
-                turned = gc[core, half * 2 + t].reshape(64, 128).astype(F32).T.astype(jnp.int32)
-                codes[pl.ds(pl.multiple_of(32 * s, 32), 32), :] = jnp.concatenate(
-                    [turned[0:32, :], turned[32:64, :]], axis=1
-                )
+            for s in range(4):
+                part = scores[:, 128 * (s // 2) : 128 * (s // 2) + 128]
+                if s % 2 != h:
+                    part = pltpu.roll(part, 64, axis=1)
                 for j in range(64):
-                    row = pl.multiple_of(j * 64 + s * 8, 8)
-                    prod[pl.ds(row, 8), :] = scores[8 * j : 8 * j + 8, 128 * t : 128 * t + 128]
-
-    score(c)
-    for n in range(5):
-        take(whole[n].at[1 - c], cr.at[n])
-    score(1 - c)
-
+                    row = pl.multiple_of(j * 64 + (core * 4 + s) * 8, 8)
+                    prod[pl.ds(row, 8), 64 * h : 64 * h + 64] = part[
+                        8 * j : 8 * j + 8, 64 * h : 64 * h + 64
+                    ]
+
+    score(0)
+    pass_second((4, 2, 3))
+    score(1)
+    for s in range(4):
+        turned = gc[s].reshape(64, 128).astype(F32).T.astype(jnp.int32)
+        turned = jnp.concatenate([turned[0:32, :], turned[32:64, :]], axis=1)
+        codes[32 * s : 32 * s + 32, :] = turned
+        codes[32 * s + 128 : 32 * s + 160, :] = turned
     high = [codes[pl.ds(p, 8, stride=32), :] for p in range(16)]
     bits = [jnp.left_shift(jnp.int32(1), codes[pl.ds(16 + p, 8, stride=32), :]) for p in range(16)]
-
-    @pl.loop(0, 32)
-    def _(a):
-        word = jnp.zeros((8, 128), jnp.int32)
-        for p in range(16):
-            word = word | jnp.where(high[p] == a, bits[p], 0)
-        words[a] = word
+    own = lax.broadcasted_iota(jnp.int32, (8, 128), 0) < 4
+
+    @pl.loop(0, 8)
+    def _(a4):
+        for a in range(4):
+            terms = [jnp.where(high[p] == a4 * 4 + a, bits[p], 0) for p in range(16)]
+            while len(terms) > 1:
+                terms = [terms[i] | terms[i + 1] for i in range(0, len(terms), 2)]
+            words[a4 * 4 + a] = jnp.where(own, terms[0], 0)
+            words2[a4 * 4 + a] = jnp.where(own, 0, terms[0])
 
     @pl.loop(0, 16)
     def _(g):
         xs = []
         for i in range(32):
             value = prod[pl.ds(g * 256 + (i // 8) * 64 + i % 8, 8, stride=8), :]
-            which = id_ref[g * 32 + i]
-            word = words[lax.shift_right_logical(which, 5)]
-            keep = (word & jnp.left_shift(jnp.int32(1), which & 31)) != 0
-            xs.append(jnp.where(keep, value, NEG))
+            found = []
+            for row_ref, bit_ref, table in ((rows1, bits1, words), (rows2, bits2, words2)):
+                word = table[row_ref[g * 32 + i]]
+                found.append(word & bit_ref[g * 32 + i])
+            xs.append(jnp.where((found[0] | found[1]) != 0, value, NEG))
         xs = sort_desc(xs)
         for i in range(32):
             runs[g * 32 + i] = xs[i]
@@ -312,22 +353,19 @@
             run_load(runs, 256 * g), run_store(runs, 256 * g), run_store(runs2, 256 * g),
         )
 
-    def split_store(i, value):
-        csend[0, i] = value[0:4, :]
-        csend[1, i] = value[4:8, :]
-
-    merge_top(run_load(runs2, 0), run_load(runs2, 256), run_load(runs, 0), run_store(runs, 0), split_store)
-
-    remote(csend.at[1 - c, pl.ds(0, SENT)], crecv.at[pl.ds(0, SENT)], rcs.at[0], rcr.at[0], partner)
-    take(crecv.at[pl.ds(0, SENT)], rcr.at[0])
+    merge_top(
+        run_load(runs2, 0), run_load(runs2, 256), run_load(runs, 0), run_store(runs, 0), run_store(runs2, 0)
+    )
 
     def x_store(i, value):
-        xsend[pl.ds(i, 4, stride=128), :] = value
-
-    merge_top(lambda i: csend[c, i], run_load(crecv, 0), run_load(ctmp, 0), run_store(ctmp, 0), x_store)
+        xsend[pl.ds(i + (x & 1) * (127 - 2 * i), 4, stride=128), :] = value
+
+    merge_top(
+        lambda i: runs2[i, 0:4, :], lambda i: runs2[i, 4:8, :], run_load(ctmp, 0), run_store(ctmp, 0), x_store
+    )
 
     def x_rows(s):
-        return pl.ds(pl.multiple_of(s * 128, 128), SENT)
+        return pl.ds(pl.multiple_of(s * 128 + (x & 1) * (128 - SENT), 8), SENT)
 
     for k in (1, 0, 2):
         remote(
@@ -337,29 +375,19 @@
     xrecv[x_rows(x), :] = xsend[x_rows(x), :]
     take(xrecv.at[pl.ds(0, 3 * SENT)], rxr.at[0])
 
-    def pair_store(i, value):
-        apair[pl.ds(i, 2, stride=128), :] = value
-
-    merge_top(
-        lambda i: xrecv[pl.ds(i, 2, stride=128), :], lambda i: xrecv[pl.ds(256 + i, 2, stride=128), :],
-        run_load(atmp, 0), run_store(atmp, 0), pair_store,
-    )
-
-    def row_load(ref, base=0):
-        return lambda i: ref[pl.ds(base + i, 1), :]
-
-    def row_store(ref):
-        def put(i, value):
-            ref[pl.ds(i, 1), :] = value
-        return put
-
-    merge_top(row_load(apair), row_load(apair, 128), row_load(row_c), row_store(row_c), row_store(row_a))
-
-    def fold_lanes(distance):
-        row_b[...] = pltpu.roll(row_a[...], 128 - distance, axis=1)
-        merge_top(row_load(row_a), row_load(row_b), row_load(row_c), row_store(row_c), row_store(row_a))
-
-    turned = row_a[...].T
+    def blocks(ref, base=0):
+        return [ref[base + 8 * i : base + 8 * i + 8, :] for i in range(16)]
+
+    def join(xs, ys):
+        return [jnp.maximum(a, b) for a, b in zip(xs, ys)]
+
+    lane = lax.broadcasted_iota(jnp.int32, (8, 128), 1)
+    low = clean_rows(join(blocks(xrecv), blocks(xrecv, 128)))
+    high = clean_rows(join(blocks(xrecv, 256), blocks(xrecv, 384)), True)
+    up = ((lax.shift_right_logical(lane, 4) + 4 - y) & 3) >= 2
+    merged = clean_rows(join(low, high), up)
+
+    turned = jnp.concatenate(merged, axis=0).T
     for h in range(2):
         for y_ in range(4):
             for r8 in range(8):
@@ -379,17 +407,21 @@
     for n in range(64):
         row_b[2 * n : 2 * n + 2, :] = drecv[n]
     row_a[...] = row_b[...].T
+    merged = blocks(row_a)
     for distance in (64, 32, 16, 8, 4, 2):
-        fold_lanes(distance)
-    o_ref[...] = row_a[...].T[0:2, 0:K]
+        merged = join(merged, [pltpu.roll(v, 128 - distance, axis=1) for v in merged])
+        up = (lane & (distance // 2)) != 0 if distance > 2 else None
+        merged = clean_rows(merged, up)
+    o_ref[...] = jnp.concatenate(merged, axis=0).T[0:2, 0:K]
 
     drain(zbuf.at[0:15], zs.at[0])
     for n in range(5):
         group, a2 = kinds[n][0], kinds[n][1]
         drain(group(a2).at[0:3], fs.at[n])
-        drain(whole[n].at[c, 0:3], ss.at[n])
-        drain(whole[n].at[c], cs.at[n])
-    drain(crecv.at[pl.ds(0, SENT)], rcs.at[0])
+        drain(whole[n].at[0:3], ss.at[n])
+    drain(v_vm.at[1], vs.at[0])
+    drain(row_of, vs.at[1])
+    drain(bit_of, vs.at[2])
     drain(xrecv.at[pl.ds(0, 3 * SENT)], rxs.at[0])
     drain(dsend.at[0:63], rds.at[0])
 
@@ -405,31 +437,33 @@
         scratch_shapes=[
             pltpu.VMEM((2, 768), jnp.bfloat16),
             pltpu.VMEM((2, 16), jnp.int32),
+            pltpu.VMEM((512,), jnp.int32),
+            pltpu.VMEM((512,), jnp.int32),
+            pltpu.VMEM((512,), jnp.int32),
+            pltpu.SMEM((512,), jnp.int32),
+            pltpu.SMEM((512,), jnp.int32),
+            pltpu.SMEM((512,), jnp.int32),
             pltpu.SMEM((512,), jnp.int32),
             pltpu.VMEM((16, 16, 128), jnp.bfloat16),
-            pltpu.VMEM((2, 2, 4, 4, 16, 384), jnp.bfloat16),
-            pltpu.VMEM((2, 2, 4, 4, 16, 384), jnp.bfloat16),
-            pltpu.VMEM((2, 4, 4, 16, 128), jnp.bfloat16),
-            pltpu.VMEM((512, 768), jnp.bfloat16),
+            pltpu.VMEM((2, 4, 4, 16, 384), jnp.bfloat16),
+            pltpu.VMEM((2, 4, 4, 16, 384), jnp.bfloat16),
+            pltpu.VMEM((4, 4, 16, 128), jnp.bfloat16),
+            pltpu.VMEM((2, 512, 768), jnp.bfloat16),
             pltpu.VMEM((4096, 128), F32),
+            pltpu.VMEM((32, 8, 128), jnp.int32),
             pltpu.VMEM((32, 8, 128), jnp.int32),
             pltpu.VMEM((256, 128), jnp.int32),
             pltpu.VMEM((512, 8, 128), F32),
             pltpu.VMEM((512, 8, 128), F32),
-            pltpu.VMEM((2, 128, 4, 128), F32),
-            pltpu.VMEM((128, 4, 128), F32),
             pltpu.VMEM((128, 4, 128), F32),
             pltpu.VMEM((512, 128), F32),
             pltpu.VMEM((512, 128), F32),
-            pltpu.VMEM((128, 2, 128), F32),
-            pltpu.VMEM((256, 128), F32),
-            pltpu.VMEM((128, 128), F32),
             pltpu.VMEM((128, 128), F32),
             pltpu.VMEM((128, 128), F32),
             pltpu.VMEM((64, 2, 128), F32),
             pltpu.VMEM((64, 2, 128), F32),
-            dma((4,)), dma((1,)), dma((1,)), dma((5,)), dma((5,)), dma((5, 3)), dma((5,)), dma((5, 3)),
-            dma((5,)), dma((5,)), dma((1,)), dma((1,)), dma((1,)), dma((1,)), dma((1,)), dma((1,)),
+            dma((6,)), dma((1,)), dma((3,)), dma((3,)), dma((1,)), dma((5,)), dma((5,)), dma((5, 3)), dma((5,)),
+            dma((5, 3)), dma((1,)), dma((1,)), dma((1,)), dma((1,)),
         ],
         compiler_params=pltpu.CompilerParams(collective_id=0, has_side_effects=True),
     )(queries, probes, vectors, list_ids)

time: 57 us -> 51.9 us (0.911)
  the two profiles are of different devices: /device:TPU:1 before, /device:TPU:8 now
where the time goes in v4:
time: 51.9 us; the launch traced here: 51.8 us
  Pallas kernels  50.5 us (97%)
  local copies, waits for them, and re-layouts  1.24 us (2%)
    pallas_call x1, Pallas kernels, local(): pl.pallas_call(kernel, out_shape=jax.ShapeDtypeStruct((2, K), F32), in_sp...  50.5 us
    unnamed x1, local copies, waits for them, and re-layouts  1.24 us

profile of v4, /device:TPU:8, one launch (start us, length us, event | category | flops | bytes accessed | tf_op | source)
XLA Modules:
  0.0 51.8 jit_solution(13781461580230989958)
XLA Ops:
  0.0 50.5 %shard_map.46 = f32[2,100]{1,0:T(2,128)} custom-call(bf16[2,768]{1,0:T(2,128)(2,1)} %q_hbm.1, s32[2,16]{1,0:T(2,128)} %p_hbm.1, bf16[512,768]{1,0:T(8,128)(2,1)} %v_hbm.1, s32[512]{0:T(512)} %id_hbm.1), custom_call_target="tpu_custom_call" | custom-call | tf_op jit(solution)/shard_map/pallas_call | solution.py:432
  50.5 1.2 %copy.6 = f32[2,100]{1,0:T(2,128)} copy(f32[2,100]{1,0:T(2,128)} %shard_map.46) | data formatting | bytes 1600

commit v5 on v4

--- a/solution.py
+++ b/solution.py
@@ -77,11 +77,11 @@
     return xs
 
 
-def merge_top(load_a, load_b, tmp_load, tmp_store, store):
-    @pl.loop(0, 8)
+def merge_top(load_a, load_b, tmp_load, tmp_store, store, after=None):
+    @pl.loop(0, 2)
     def _(g):
-        for u in range(4):
-            i = g * 4 + u
+        for u in range(16):
+            i = g * 16 + u
             m = [jnp.maximum(load_a(i + 32 * k), load_b(127 - i - 32 * k)) for k in range(4)]
             m[0], m[2] = exchange(m[0], m[2])
             m[1], m[3] = exchange(m[1], m[3])
@@ -90,16 +90,22 @@
             for k in range(4):
                 tmp_store(i + 32 * k, m[k])
 
-    @pl.loop(0, 4)
-    def _(k):
+    def finish(k):
         xs = clean_desc([tmp_load(32 * k + i) for i in range(32)])
         for i in range(32):
             store(32 * k + i, xs[i])
 
+    if after is None:
+        pl.loop(0, 4)(finish)
+    else:
+        for k in range(4):
+            finish(k)
+            after(k)
+
 
 def kernel(
-    q_hbm, p_hbm, v_hbm, id_hbm, o_ref,
-    q_ref, p_ref, ids, row_of, bit_of, rows1, bits1, rows2, bits2, zbuf, ga, gb, gc, v_vm, prod, words, words2, codes, runs, runs2, ctmp,
+    q_hbm, p_hbm, v_hbm, id_hbm, flat_hbm, o_ref,
+    q_ref, p_ref, ids, ids2, flat, row_of, rows1, rows2, bit_of, zbuf, ga, gb, gc, v_vm, prod, words, words2, codes, runs, runs2, ctmp,
     xsend, xrecv, row_a, row_b, dsend, drecv,
     in_sem, done, vs, vr, zs, zr, fs, fr, ss, sr, rxs, rxr, rds, rdr,
 ):
@@ -125,7 +131,7 @@
     fetch = [
         pltpu.make_async_copy(src, dst, in_sem.at[n])
         for n, (src, dst) in enumerate(
-            ((q_hbm, q_ref), (p_hbm, p_ref), (id_hbm, ids), (v_hbm, v_vm.at[0]))
+            ((q_hbm, q_ref), (p_hbm, p_ref), (id_hbm, ids), (v_hbm, v_vm.at[0]), (flat_hbm, flat))
         )
     ]
     for copy in fetch:
@@ -171,15 +177,12 @@
         z_send(0, k, min(k, 16 - k))
     remote(v_hbm, v_vm.at[1], vs.at[0], vr.at[0], partner)
     fetch[2].wait()
-    row_of[...] = lax.shift_right_logical(ids[...], 5)
-    bit_of[...] = jnp.left_shift(jnp.int32(1), ids[...] & 31)
-    tables = [
-        pltpu.make_async_copy(row_of, rows1, in_sem.at[4]), pltpu.make_async_copy(bit_of, bits1, in_sem.at[5])
-    ]
-    for copy in tables:
-        copy.start()
+    fetch[4].wait()
+    row_of[...] = lax.shift_right_logical(flat[...], 5)
+    table = pltpu.make_async_copy(row_of, rows1, in_sem.at[5])
+    table.start()
     remote(row_of, rows2, vs.at[1], vr.at[1], partner)
-    remote(bit_of, bits2, vs.at[2], vr.at[2], partner)
+    remote(ids, ids2, vs.at[2], vr.at[2], partner)
     r = lax.broadcasted_iota(jnp.int32, (112, 128), 0)
     k_ = lax.broadcasted_iota(jnp.int32, (112, 128), 1)
     pick = k_ == lax.shift_right_logical(r & 15, 1) * 16 + lax.shift_right_logical(r, 4) * 2 + (r & 1)
@@ -238,6 +241,15 @@
             z_send(j, 12, 0)
     near_codes = place(0)
     start((0, 1))
+
+    take(ids2, vr.at[2])
+    for part in range(4):
+        for s, ref in enumerate((ids, ids2)):
+            column = jnp.broadcast_to(ref[part : part + 1, :], (128, 128)).T
+            bit = jnp.left_shift(jnp.int32(1), column & 31)
+            for t in range(4):
+                bit_of[pl.ds(part * 1024 + 4 * s + t, 128, stride=8), :] = bit
+
     take(zbuf.at[0:7], zr.at[0])
     far_codes = place(1)
     gc[x, y] = (near_codes + pltpu.roll(far_codes, 32, axis=1)).astype(jnp.bfloat16)
@@ -246,11 +258,9 @@
     pass_first((4, 2, 3))
     pass_second((0, 1))
     fetch[3].wait()
-    for copy in tables:
-        copy.wait()
+    table.wait()
     take(v_vm.at[1], vr.at[0])
     take(rows2, vr.at[1])
-    take(bits2, vr.at[2])
 
     def score(h):
         block = jnp.concatenate(
@@ -277,8 +287,7 @@
                     ]
 
     score(0)
-    pass_second((4, 2, 3))
-    score(1)
+    pass_second((4,))
     for s in range(4):
         turned = gc[s].reshape(64, 128).astype(F32).T.astype(jnp.int32)
         turned = jnp.concatenate([turned[0:32, :], turned[32:64, :]], axis=1)
@@ -297,16 +306,17 @@
             words[a4 * 4 + a] = jnp.where(own, terms[0], 0)
             words2[a4 * 4 + a] = jnp.where(own, 0, terms[0])
 
+    pass_second((2, 3))
+    score(1)
+
     @pl.loop(0, 16)
     def _(g):
         xs = []
         for i in range(32):
             value = prod[pl.ds(g * 256 + (i // 8) * 64 + i % 8, 8, stride=8), :]
-            found = []
-            for row_ref, bit_ref, table in ((rows1, bits1, words), (rows2, bits2, words2)):
-                word = table[row_ref[g * 32 + i]]
-                found.append(word & bit_ref[g * 32 + i])
-            xs.append(jnp.where((found[0] | found[1]) != 0, value, NEG))
+            word = words[rows1[g * 32 + i]] | words2[rows2[g * 32 + i]]
+            found = word & bit_of[pl.ds(pl.multiple_of(g * 256 + i * 8, 8), 8), :]
+            xs.append(jnp.where(found != 0, value, NEG))
         xs = sort_desc(xs)
         for i in range(32):
             runs[g * 32 + i] = xs[i]
@@ -360,19 +370,23 @@
     def x_store(i, value):
         xsend[pl.ds(i + (x & 1) * (127 - 2 * i), 4, stride=128), :] = value
 
+    def x_rows(s, start, size):
+        ascending = 128 - size - start
+        return pl.ds(pl.multiple_of(s * 128 + start + (x & 1) * (ascending - start), 8), size)
+
+    def x_send(q):
+        start, size = 32 * q, min(32, SENT - 32 * q)
+        for k in (1, 0, 2):
+            remote(
+                xsend.at[x_rows((x + k + 1) % 4, start, size)], xrecv.at[x_rows(x, start, size)],
+                rxs.at[0], rxr.at[0], x_peers[k],
+            )
+
     merge_top(
-        lambda i: runs2[i, 0:4, :], lambda i: runs2[i, 4:8, :], run_load(ctmp, 0), run_store(ctmp, 0), x_store
+        lambda i: runs2[i, 0:4, :], lambda i: runs2[i, 4:8, :], run_load(ctmp, 0), run_store(ctmp, 0), x_store,
+        x_send,
     )
-
-    def x_rows(s):
-        return pl.ds(pl.multiple_of(s * 128 + (x & 1) * (128 - SENT), 8), SENT)
-
-    for k in (1, 0, 2):
-        remote(
-            xsend.at[x_rows((x + k + 1) % 4)], xrecv.at[x_rows(x)],
-            rxs.at[0], rxr.at[0], x_peers[k],
-        )
-    xrecv[x_rows(x), :] = xsend[x_rows(x), :]
+    xrecv[x_rows(x, 0, SENT), :] = xsend[x_rows(x, 0, SENT), :]
     take(xrecv.at[pl.ds(0, 3 * SENT)], rxr.at[0])
 
     def blocks(ref, base=0):
@@ -420,8 +434,8 @@
         drain(group(a2).at[0:3], fs.at[n])
         drain(whole[n].at[0:3], ss.at[n])
     drain(v_vm.at[1], vs.at[0])
-    drain(row_of, vs.at[1])
-    drain(bit_of, vs.at[2])
+    drain(rows2, vs.at[1])
+    drain(ids2, vs.at[2])
     drain(xrecv.at[pl.ds(0, 3 * SENT)], rxs.at[0])
     drain(dsend.at[0:63], rds.at[0])
 
@@ -432,18 +446,18 @@
     return pl.pallas_call(
         kernel,
         out_shape=jax.ShapeDtypeStruct((2, K), F32),
-        in_specs=[pl.BlockSpec(memory_space=pltpu.HBM)] * 4,
+        in_specs=[pl.BlockSpec(memory_space=pltpu.HBM)] * 5,
         out_specs=vmem,
         scratch_shapes=[
             pltpu.VMEM((2, 768), jnp.bfloat16),
             pltpu.VMEM((2, 16), jnp.int32),
-            pltpu.VMEM((512,), jnp.int32),
+            pltpu.VMEM((4, 128), jnp.int32),
+            pltpu.VMEM((4, 128), jnp.int32),
             pltpu.VMEM((512,), jnp.int32),
             pltpu.VMEM((512,), jnp.int32),
             pltpu.SMEM((512,), jnp.int32),
             pltpu.SMEM((512,), jnp.int32),
-            pltpu.SMEM((512,), jnp.int32),
-            pltpu.SMEM((512,), jnp.int32),
+            pltpu.VMEM((4096, 128), jnp.int32),
             pltpu.VMEM((16, 16, 128), jnp.bfloat16),
             pltpu.VMEM((2, 4, 4, 16, 384), jnp.bfloat16),
             pltpu.VMEM((2, 4, 4, 16, 384), jnp.bfloat16),
@@ -466,7 +480,7 @@
             dma((5, 3)), dma((1,)), dma((1,)), dma((1,)), dma((1,)),
         ],
         compiler_params=pltpu.CompilerParams(collective_id=0, has_side_effects=True),
-    )(queries, probes, vectors, list_ids)
+    )(queries, probes, vectors, list_ids.reshape(4, 128), list_ids)
 
 
 def solution(mesh):

time: 51.9 us -> 51.3 us (0.988)
  Pallas kernels: 50.5 us -> 49.9 us
    pallas_call x1, Pallas kernels: 50.5 us -> 49.9 us  [local(): pl.pallas_call(kernel, out_shape=jax.ShapeDtypeStruct((2, K), F32), in_sp...]
where the time goes in v5:
time: 51.3 us; the launch traced here: 51.2 us
  Pallas kernels  49.9 us (97%)
  local copies, waits for them, and re-layouts  1.24 us (2%)
    pallas_call x1, Pallas kernels, local(): pl.pallas_call(kernel, out_shape=jax.ShapeDtypeStruct((2, K), F32), in_sp...  49.9 us
    unnamed x1, local copies, waits for them, and re-layouts  1.24 us

profile of v5, /device:TPU:8, one launch (start us, length us, event | category | flops | bytes accessed | tf_op | source)
XLA Modules:
  0.0 51.2 jit_solution(12008302955689434488)
XLA Ops:
  0.0 49.9 %shard_map.46 = f32[2,100]{1,0:T(2,128)} custom-call(bf16[2,768]{1,0:T(2,128)(2,1)} %q_hbm.1, s32[2,16]{1,0:T(2,128)} %p_hbm.1, bf16[512,768]{1,0:T(8,128)(2,1)} %v_hbm.1, s32[4,128]{1,0:T(4,128)} %bitcast.1, s32[512]{0:T(512)} %flat_hbm.1), custom_call_target="tpu_custom_call" | custom-call | tf_op jit(solution)/shard_map/pallas_call | solution.py:446
  49.9 1.2 %copy.6 = f32[2,100]{1,0:T(2,128)} copy(f32[2,100]{1,0:T(2,128)} %shard_map.46) | data formatting | bytes 1600

commit v6 on v5

--- a/solution.py
+++ b/solution.py
@@ -479,7 +479,7 @@
             dma((6,)), dma((1,)), dma((3,)), dma((3,)), dma((1,)), dma((5,)), dma((5,)), dma((5, 3)), dma((5,)),
             dma((5, 3)), dma((1,)), dma((1,)), dma((1,)), dma((1,)),
         ],
-        compiler_params=pltpu.CompilerParams(collective_id=0, has_side_effects=True),
+        compiler_params=pltpu.CompilerParams(collective_id=0, has_side_effects=True, vmem_limit_bytes=56550000),
     )(queries, probes, vectors, list_ids.reshape(4, 128), list_ids)
 
 

time: 51.3 us -> 50 us (0.975)
  local copies, waits for them, and re-layouts: 1.24 us -> 0.56 us
  Pallas kernels: 49.9 us -> 49.3 us
    unnamed x1, local copies, waits for them, and re-layouts: 1.24 us -> 0.56 us
    pallas_call x1, Pallas kernels: 49.9 us -> 49.3 us  [local(): pl.pallas_call(kernel, out_shape=jax.ShapeDtypeStruct((2, K), F32), in_sp...]
where the time goes in v6:
time: 50 us; the launch traced here: 49.9 us
  Pallas kernels  49.3 us (99%)
  local copies, waits for them, and re-layouts  0.56 us (1%)
    pallas_call x1, Pallas kernels, local(): pl.pallas_call(kernel, out_shape=jax.ShapeDtypeStruct((2, K), F32), in_sp...  49.3 us

profile of v6, /device:TPU:8, one launch (start us, length us, event | category | flops | bytes accessed | tf_op | source)
XLA Modules:
  0.0 49.9 jit_solution(6663094895641948642)
XLA Ops:
  0.0 49.3 %shard_map.46 = f32[2,100]{1,0:T(2,128)S(1)} custom-call(bf16[2,768]{1,0:T(2,128)(2,1)} %q_hbm.1, s32[2,16]{1,0:T(2,128)} %p_hbm.1, bf16[512,768]{1,0:T(8,128)(2,1)} %v_hbm.1, s32[4,128]{1,0:T(4,128)} %bitcast.1, s32[512]{0:T(512)} %flat_hbm.1), custom_call_target="tpu_custom_call" | custom-call | tf_op jit(solution)/shard_map/pallas_call | solution.py:446
  49.3 0.6 %copy.6 = f32[2,100]{1,0:T(2,128)} copy(f32[2,100]{1,0:T(2,128)S(1)} %shard_map.46) | data formatting | bytes 1600

commit v7 on v6

--- a/solution.py
+++ b/solution.py
@@ -96,7 +96,10 @@
             store(32 * k + i, xs[i])
 
     if after is None:
-        pl.loop(0, 4)(finish)
+        @pl.loop(0, 2)
+        def _(pair):
+            finish(pair * 2)
+            finish(pair * 2 + 1)
     else:
         for k in range(4):
             finish(k)
@@ -343,11 +346,12 @@
             runs[base + i], runs[base + 32 + i] = h1, h2
             runs[base + 64 + i], runs[base + 96 + i] = l1, l2
 
-    @pl.loop(0, 16)
-    def _(g):
-        xs = clean_desc([runs[g * 32 + i] for i in range(32)])
-        for i in range(32):
-            runs2[g * 32 + i] = xs[i]
+    @pl.loop(0, 8)
+    def _(pair):
+        for g in (pair * 2, pair * 2 + 1):
+            xs = clean_desc([runs[g * 32 + i] for i in range(32)])
+            for i in range(32):
+                runs2[g * 32 + i] = xs[i]
 
     def run_store(ref, base):
         def put(i, value):

time: 50 us -> 49.9 us (level)
  no operation moved by 1% of the time
where the time goes in v7:
time: 49.9 us; the launch traced here: 49.8 us
  Pallas kernels  49.2 us (99%)
  local copies, waits for them, and re-layouts  0.56 us (1%)
    pallas_call x1, Pallas kernels, local(): pl.pallas_call(kernel, out_shape=jax.ShapeDtypeStruct((2, K), F32), in_sp...  49.2 us

profile of v7, /device:TPU:8, one launch (start us, length us, event | category | flops | bytes accessed | tf_op | source)
XLA Modules:
  0.0 49.8 jit_solution(1649409577210765143)
XLA Ops:
  0.0 49.2 %shard_map.46 = f32[2,100]{1,0:T(2,128)S(1)} custom-call(bf16[2,768]{1,0:T(2,128)(2,1)} %q_hbm.1, s32[2,16]{1,0:T(2,128)} %p_hbm.1, bf16[512,768]{1,0:T(8,128)(2,1)} %v_hbm.1, s32[4,128]{1,0:T(4,128)} %bitcast.1, s32[512]{0:T(512)} %flat_hbm.1), custom_call_target="tpu_custom_call" | custom-call | tf_op jit(solution)/shard_map/pallas_call | solution.py:450
  49.2 0.6 %copy.6 = f32[2,100]{1,0:T(2,128)} copy(f32[2,100]{1,0:T(2,128)S(1)} %shard_map.46) | data formatting | bytes 1600
